TPU v7x, 256 devices: a whole 4x4x8 slice. The times are simulated.
256 devices in a mesh: dx: 8 (over x, z_hi), dy: 32 (over y, z_lo, core).
Axes of the slice: x: 4, y: 4, z: 8 (z_hi: 2, z_lo: 4; z = z_hi * 4 + z_lo), core: 2. Of those that a mesh axis runs over, the one named last changes fastest.
Arguments:
- seg_mid: float32 [8, 32, 3, 4096], P('dx', 'dy'), may hold values from 0 to 1
- seg_line: float32 [8, 32, 3, 4096], P('dx', 'dy'), may hold values from -0.3 to 0.3
- seg_burgers: float32 [8, 32, 3, 4096], P('dx', 'dy'), may hold values from -5 to 5
- seg_cell: int32 [8, 32, 4096], P('dx', 'dy'), may hold values from 0 to 71, as said below
- seg_node: int32 [8, 32, 2, 4096], P('dx', 'dy'), may hold values from 0 to 4607, as said below
- ghost_list: int32 [8, 32, 8, 2], P('dx', 'dy'), may hold values from 0 to 31
- ghost_count: int32 [8, 32, 8], P('dx', 'dy'), may hold values from 1 to 2
- pair_list: int32 [8, 32, 32, 12], P('dx', 'dy'), may hold values from 0 to 47, as said below
- pair_count: int32 [8, 32, 32], P('dx', 'dy'), may hold values from 1 to 12
Outputs:
- node_force: float32 [8, 32, 3, 512], P('dx', 'dy')
- cell_moments: float32 [315, 2048], P(None, ('dx', 'dy'))
Inputs may be any that keep to these rules, and one draw needn't show every extreme that they name: `seg_node`: each entry is d * 512 + m with m a node of the domain at offset (a, b) from the segment's domain, d = 3 (a + 1) + (b + 1), a and b in -1, 0, 1; d = 4 is the domain itself. `seg_cell`: each entry is d * 8 + c with c a cell owned by the domain at offset (a, b) from the segment's domain, d = 3 (a + 1) + (b + 1), a and b in -1, 0, 1; d = 4 is the domain itself. `pair_list`: the entries of one tile's list are distinct.
All inputs are finite; a program needn't handle non-finite values.
Results may differ from a plain program's by a relative error of at most 0.0003.
Values sent between devices are 32-bit elements; how exact they have to be, the bound alone decides.
A program may use at most 64 MiB of HBM per device.

v0:
```python
import jax
import jax.numpy as jnp
import numpy as np
from jax import lax
from jax.sharding import PartitionSpec as P

TILE = 128
GHOST = 2
NP = 12
NODE_DEV = 512
CELL_DEV = 8


core_radius = 0.1
shear_scale = 0.25
highest = lax.Precision.HIGHEST
neighbour_offsets = ((-1, -1), (-1, 0), (-1, 1), (0, -1), (0, 1), (1, -1), (1, 0), (1, 1))


def passed_along(block, axis, distance):
    devices = range(lax.axis_size(axis))
    route = [((i - distance) % len(devices), i) for i in devices]
    return lax.ppermute(block, axis, route)


def exponent_table():
    exponent_rows = []
    for degree in range(5):
        for first_power in range(degree, -1, -1):
            for second in range(degree - first_power, -1, -1):
                exponent_rows.append((first_power, second, degree - first_power - second))
    return np.array(exponent_rows, dtype=np.int32)


def moment_terms(midpoint, line_vector, burgers):
    scaled = 2.0 * (midpoint - 0.5)
    powers = jnp.stack(
        [jnp.ones_like(scaled), scaled, scaled * scaled, scaled**3, scaled**4], axis=1
    )
    exponents = exponent_table()
    monomial = powers[0, exponents[:, 0]] * powers[1, exponents[:, 1]] * powers[2, exponents[:, 2]]
    products = (burgers[:, None, :] * line_vector[None, :, :]).reshape(9, -1)
    return (products[:, None, :] * monomial[None, :, :]).reshape(9 * monomial.shape[0], -1)


def pair_stress(field_tiles, source_tiles, valid_weight):
    separation = [
        field_tiles[component][:, :, None] - source_tiles[component][:, None, :]
        for component in range(3)
    ]
    line_source = source_tiles[3:6]
    burgers_source = source_tiles[6:9]
    cross_source = [
        burgers_source[1] * line_source[2] - burgers_source[2] * line_source[1],
        burgers_source[2] * line_source[0] - burgers_source[0] * line_source[2],
        burgers_source[0] * line_source[1] - burgers_source[1] * line_source[0],
    ]
    cross_source = [entry_value[:, None, :] for entry_value in cross_source]
    radius_sq = separation[0] ** 2 + separation[1] ** 2 + separation[2] ** 2 + core_radius**2
    inverse = 1.0 / jnp.sqrt(radius_sq)
    weight = shear_scale * valid_weight[:, None, None] * inverse / radius_sq
    projection = (
        separation[0] * cross_source[0]
        + separation[1] * cross_source[1]
        + separation[2] * cross_source[2]
    )
    diagonal_term = projection * (1.0 + 1.5 * core_radius**2 / radius_sq)
    entries = []
    for first_axis, second_axis in ((0, 0), (1, 1), (2, 2), (0, 1), (0, 2), (1, 2)):
        entry_value = (
            separation[first_axis] * cross_source[second_axis]
            + separation[second_axis] * cross_source[first_axis]
            - 3.0 * projection * separation[first_axis] * separation[second_axis] / radius_sq
        )
        if first_axis == second_axis:
            entry_value = entry_value + diagonal_term
        entries.append(jnp.sum(weight * entry_value, axis=2))
    return jnp.stack(entries)


def segment_force(stress, own_columns):
    line_vector = own_columns[3:6]
    burgers = own_columns[6:9]
    traction = [
        stress[0] * burgers[0] + stress[3] * burgers[1] + stress[4] * burgers[2],
        stress[3] * burgers[0] + stress[1] * burgers[1] + stress[5] * burgers[2],
        stress[4] * burgers[0] + stress[5] * burgers[1] + stress[2] * burgers[2],
    ]
    return jnp.stack(
        [
            traction[1] * line_vector[2] - traction[2] * line_vector[1],
            traction[2] * line_vector[0] - traction[0] * line_vector[2],
            traction[0] * line_vector[1] - traction[1] * line_vector[0],
        ]
    )


def on_device(
    seg_mid,
    seg_line,
    seg_burgers,
    seg_cell,
    seg_node,
    ghost_list,
    ghost_count,
    pair_list,
    pair_count,
):
    seg_data = jnp.concatenate([seg_mid[0, 0], seg_line[0, 0], seg_burgers[0, 0]], axis=0)
    own_count = seg_data.shape[1] // TILE
    own_tiles = seg_data.reshape(9, own_count, TILE).transpose(1, 0, 2)
    packets = own_tiles[ghost_list[0, 0]]
    slot_valid = (jnp.arange(GHOST, dtype=jnp.int32)[None, :] < ghost_count[0, 0][:, None]).astype(
        jnp.float32
    )
    packets = packets * slot_valid[:, :, None, None]
    along_x = [
        passed_along(outgoing, "dx", stride)
        for stride, outgoing in ((1, packets[5:8]), (-1, packets[0:3]))
    ]
    from_left = along_x[0]
    from_right = along_x[1]
    upward = jnp.stack([packets[4], from_left[2], from_right[2]])
    downward = jnp.stack([packets[3], from_left[0], from_right[0]])
    along_y = [
        passed_along(outgoing, "dy", stride) for stride, outgoing in ((1, upward), (-1, downward))
    ]
    from_below = along_y[0]
    from_above = along_y[1]
    terms = moment_terms(seg_mid[0, 0], seg_line[0, 0], seg_burgers[0, 0])
    cell_columns = jnp.arange(9 * CELL_DEV, dtype=jnp.int32)
    membership = (seg_cell[0, 0][:, None] == cell_columns[None, :]).astype(jnp.float32)
    moment_partial = jnp.dot(
        terms, membership, precision=highest, preferred_element_type=jnp.float32
    )
    cell_grid = moment_partial.reshape(moment_partial.shape[0], 3, 3, CELL_DEV)
    cell_rows = [
        passed_along(cell_grid[:, :, column], "dy", stride) for stride, column in ((1, 2), (-1, 0))
    ]
    cell_middle = cell_grid[:, :, 1] + cell_rows[0] + cell_rows[1]
    cell_cols = [
        passed_along(cell_middle[:, column], "dx", stride) for stride, column in ((1, 2), (-1, 0))
    ]
    cell_moments = cell_middle[:, 1] + cell_cols[0] + cell_cols[1]
    groups = [
        from_below[1],
        from_left[1],
        from_above[1],
        from_below[0],
        from_above[0],
        from_below[2],
        from_right[1],
        from_above[2],
    ]
    shifted = []
    for group_index in range(8):
        first_shift, second_shift = neighbour_offsets[group_index]
        offset_rows = jnp.array([first_shift, second_shift, 0, 0, 0, 0, 0, 0, 0], jnp.float32)
        shifted.append(groups[group_index] + offset_rows[None, :, None])
    source_pool = jnp.concatenate([own_tiles] + shifted, axis=0)
    own_columns = own_tiles.transpose(1, 0, 2)
    pair_rows = pair_list[0, 0]
    pair_limit = pair_count[0, 0]

    def add_slot(stress_total, slot_index):
        source_tiles = source_pool[pair_rows[:, slot_index]].transpose(1, 0, 2)
        valid_weight = (slot_index < pair_limit).astype(jnp.float32)
        return (stress_total + pair_stress(own_columns, source_tiles, valid_weight), None)

    stress_total, unused = lax.scan(
        add_slot, jnp.zeros((6, own_count, TILE), jnp.float32), jnp.arange(NP, dtype=jnp.int32)
    )
    force = segment_force(stress_total, own_columns).reshape(3, own_count * TILE)
    node_columns = jnp.arange(9 * NODE_DEV, dtype=jnp.int32)
    node_ends = seg_node[0, 0]
    incidence = (node_ends[0][:, None] == node_columns[None, :]).astype(jnp.float32) + (
        node_ends[1][:, None] == node_columns[None, :]
    ).astype(jnp.float32)
    node_partial = jnp.dot(
        0.5 * force, incidence, precision=highest, preferred_element_type=jnp.float32
    )
    node_grid = node_partial.reshape(3, 3, 3, NODE_DEV)
    along_rows = [
        passed_along(node_grid[:, row], "dx", stride) for stride, row in ((1, 2), (-1, 0))
    ]
    partial_mid = node_grid[:, 1] + along_rows[0] + along_rows[1]
    along_cols = [
        passed_along(partial_mid[:, column], "dy", stride) for stride, column in ((1, 2), (-1, 0))
    ]
    node_total = partial_mid[:, 1] + along_cols[0] + along_cols[1]
    return (node_total[None, None], cell_moments)


def solution(mesh):
    in_specs = (
        P("dx", "dy", None, None),
        P("dx", "dy", None, None),
        P("dx", "dy", None, None),
        P("dx", "dy", None),
        P("dx", "dy", None, None),
        P("dx", "dy", None, None),
        P("dx", "dy", None),
        P("dx", "dy", None, None),
        P("dx", "dy", None),
    )
    out_specs = (P("dx", "dy", None, None), P(None, ("dx", "dy")))
    return jax.shard_map(
        on_device, mesh=mesh, in_specs=in_specs, out_specs=out_specs, check_vma=False
    )
```

profile of v0, /device:TPU:1, one launch (start us, length us, event | category | flops | bytes accessed | tf_op | source)
XLA Modules:
  0.0 280.9 jit_solution(677629236617644176)
XLA Ops:
  3.9 7.8 %collective-permute-start = (f32[3,2,9,128]{3,2,1,0:T(8,128)S(1)}, f32[3,2,9,128]{3,2,1,0:T(8,128)S(1)}, u32[]{:S(2)}, u32[]{:S(2)}) collective-permute-start(f32[3,2,9,128]{3,2,1,0:T(8,128)S(1)} %get-tuple-element.106), channel_id=1, source_target_pairs={{224,0},{0,32},{32,64},{64,96},{96,128},{128,160},{160,192},{192,2... | collective-permute-start | bytes 82952 | tf_op jit(solution)/shard_map/ppermute | solution.py:23
  11.7 2.3 collective-permute-start.1
  24.0 3.3 %broadcast_multiply_fusion = f32[9,35,4096]{2,1,0:T(8,128)} fusion(f32[35,4096]{1,0:T(8,128)S(1)} %multiply_multiply_fusion, f32[9,4096]{1,0:T(8,128)S(1)} %mul.423), kind=kLoop, calls=%fused_computation.95 | loop fusion | flops 1290240 | bytes 5881856 | tf_op jit(solution)/shard_map/mul | solution.py:43
  27.2 7.3 %reshape.357 = f32[315,4096,1,1]{1,0,2,3:T(8,128)} reshape(f32[9,35,4096]{2,1,0:T(8,128)} %broadcast_multiply_fusion) | data formatting | bytes 10321920 | tf_op jit(solution)/shard_map/mul | solution.py:43
  34.6 5.3 %fusion.50 = f32[315,3,3,8]{0,3,2,1:T(8,128)S(1)} fusion(f32[315,4096,1,1]{1,0,2,3:T(8,128)} %reshape.357, s32[3,3,8]{2,1,0:T(4,128)S(1)} %multiply_add_fusion.4, s32[4096]{0:T(1024)S(1)} %bitcast.234), kind=kOutput, calls=%fused_computation.93 | convolution fusion | flops 1115062272 | bytes 5268352 | tf_op jit(solution)/shard_map/dot_general | solution.py:133
  43.7 3.8 %collective-permute-start.3 = (f32[3,2,9,128]{3,2,1,0:T(8,128)S(1)}, f32[3,2,9,128]{3,2,1,0:T(8,128)S(1)}, u32[]{:S(2)}, u32[]{:S(2)}) collective-permute-start(f32[3,2,9,128]{3,2,1,0:T(8,128)S(1)} %pad_maximum_fusion.2), channel_id=1, source_target_pairs={{1,0},{2,1},{3,2},{4,3},{5,4},{6,5},{7,6},{8,7},{9,8},{10,9},{11,1... | collective-permute-start | bytes 82952 | tf_op jit(solution)/shard_map/ppermute | solution.py:23
  48.9 139.4 %while.11 = (s32[]{:T(128)}, f32[6,32,128]{2,1,0:T(8,128)S(1)}, f32[9,32,128]{2,1,0:T(8,128)S(1)}, s32[12]{0:T(128)S(1)}, s32[32,12]{0,1:T(8,128)S(1)}, /*index=...) while((s32[]{:T(128)}, f32[6,32,128]{2,1,0:T(8,128)S(1)}, ...), condition=%wide.region_7.8_spmd.clone, body=%wide.region_0.7_spmd.clone.sunk | while | flops 35714212 | bytes 1381413 | solution.py:170
  52.9 7.5 %fusion.99 = (f32[32,128]{1,0:T(8,128)S(1)}, f32[32,128]{1,0:T(8,128)S(1)}, f32[32,128]{1,0:T(8,128)S(1)}, f32[32,128]{1,0:T(8,128)S(1)}, f32[32,128]{1,0:T(8,128)S(1)}, /*index=5*/f32[32,128]{1,0:T(8,128)S(1)}) fusion(f32[32,128]{1,0:T(8,128)S(1)} %bitcast.211, f32[32,128]{1,0:T(8,128)S(1)} %bitcast.210, f32[32,128]{1,0:T(8,128)S(1)} %bitcast.212, ...), kind=kLoop, calls=%fused_computation.62.clone.1 | loop fusion | flops 35627008 | bytes 245888 | tf_op jit(solution)/shard_map/while/body/eval_jaxpr/reduce_sum | solution.py:77
  64.5 7.5 %fusion.99 = (f32[32,128]{1,0:T(8,128)S(1)}, f32[32,128]{1,0:T(8,128)S(1)}, f32[32,128]{1,0:T(8,128)S(1)}, f32[32,128]{1,0:T(8,128)S(1)}, f32[32,128]{1,0:T(8,128)S(1)}, /*index=5*/f32[32,128]{1,0:T(8,128)S(1)}) fusion(f32[32,128]{1,0:T(8,128)S(1)} %bitcast.211, f32[32,128]{1,0:T(8,128)S(1)} %bitcast.210, f32[32,128]{1,0:T(8,128)S(1)} %bitcast.212, ...), kind=kLoop, calls=%fused_computation.62.clone.1 | loop fusion | flops 35627008 | bytes 245888 | tf_op jit(solution)/shard_map/while/body/eval_jaxpr/reduce_sum | solution.py:77
  76.1 7.5 %fusion.99 = (f32[32,128]{1,0:T(8,128)S(1)}, f32[32,128]{1,0:T(8,128)S(1)}, f32[32,128]{1,0:T(8,128)S(1)}, f32[32,128]{1,0:T(8,128)S(1)}, f32[32,128]{1,0:T(8,128)S(1)}, /*index=5*/f32[32,128]{1,0:T(8,128)S(1)}) fusion(f32[32,128]{1,0:T(8,128)S(1)} %bitcast.211, f32[32,128]{1,0:T(8,128)S(1)} %bitcast.210, f32[32,128]{1,0:T(8,128)S(1)} %bitcast.212, ...), kind=kLoop, calls=%fused_computation.62.clone.1 | loop fusion | flops 35627008 | bytes 245888 | tf_op jit(solution)/shard_map/while/body/eval_jaxpr/reduce_sum | solution.py:77
  87.7 7.5 %fusion.99 = (f32[32,128]{1,0:T(8,128)S(1)}, f32[32,128]{1,0:T(8,128)S(1)}, f32[32,128]{1,0:T(8,128)S(1)}, f32[32,128]{1,0:T(8,128)S(1)}, f32[32,128]{1,0:T(8,128)S(1)}, /*index=5*/f32[32,128]{1,0:T(8,128)S(1)}) fusion(f32[32,128]{1,0:T(8,128)S(1)} %bitcast.211, f32[32,128]{1,0:T(8,128)S(1)} %bitcast.210, f32[32,128]{1,0:T(8,128)S(1)} %bitcast.212, ...), kind=kLoop, calls=%fused_computation.62.clone.1 | loop fusion | flops 35627008 | bytes 245888 | tf_op jit(solution)/shard_map/while/body/eval_jaxpr/reduce_sum | solution.py:77
  99.3 7.5 %fusion.99 = (f32[32,128]{1,0:T(8,128)S(1)}, f32[32,128]{1,0:T(8,128)S(1)}, f32[32,128]{1,0:T(8,128)S(1)}, f32[32,128]{1,0:T(8,128)S(1)}, f32[32,128]{1,0:T(8,128)S(1)}, /*index=5*/f32[32,128]{1,0:T(8,128)S(1)}) fusion(f32[32,128]{1,0:T(8,128)S(1)} %bitcast.211, f32[32,128]{1,0:T(8,128)S(1)} %bitcast.210, f32[32,128]{1,0:T(8,128)S(1)} %bitcast.212, ...), kind=kLoop, calls=%fused_computation.62.clone.1 | loop fusion | flops 35627008 | bytes 245888 | tf_op jit(solution)/shard_map/while/body/eval_jaxpr/reduce_sum | solution.py:77
  110.9 7.5 %fusion.99 = (f32[32,128]{1,0:T(8,128)S(1)}, f32[32,128]{1,0:T(8,128)S(1)}, f32[32,128]{1,0:T(8,128)S(1)}, f32[32,128]{1,0:T(8,128)S(1)}, f32[32,128]{1,0:T(8,128)S(1)}, /*index=5*/f32[32,128]{1,0:T(8,128)S(1)}) fusion(f32[32,128]{1,0:T(8,128)S(1)} %bitcast.211, f32[32,128]{1,0:T(8,128)S(1)} %bitcast.210, f32[32,128]{1,0:T(8,128)S(1)} %bitcast.212, ...), kind=kLoop, calls=%fused_computation.62.clone.1 | loop fusion | flops 35627008 | bytes 245888 | tf_op jit(solution)/shard_map/while/body/eval_jaxpr/reduce_sum | solution.py:77
  122.5 7.5 %fusion.99 = (f32[32,128]{1,0:T(8,128)S(1)}, f32[32,128]{1,0:T(8,128)S(1)}, f32[32,128]{1,0:T(8,128)S(1)}, f32[32,128]{1,0:T(8,128)S(1)}, f32[32,128]{1,0:T(8,128)S(1)}, /*index=5*/f32[32,128]{1,0:T(8,128)S(1)}) fusion(f32[32,128]{1,0:T(8,128)S(1)} %bitcast.211, f32[32,128]{1,0:T(8,128)S(1)} %bitcast.210, f32[32,128]{1,0:T(8,128)S(1)} %bitcast.212, ...), kind=kLoop, calls=%fused_computation.62.clone.1 | loop fusion | flops 35627008 | bytes 245888 | tf_op jit(solution)/shard_map/while/body/eval_jaxpr/reduce_sum | solution.py:77
  134.2 7.5 %fusion.99 = (f32[32,128]{1,0:T(8,128)S(1)}, f32[32,128]{1,0:T(8,128)S(1)}, f32[32,128]{1,0:T(8,128)S(1)}, f32[32,128]{1,0:T(8,128)S(1)}, f32[32,128]{1,0:T(8,128)S(1)}, /*index=5*/f32[32,128]{1,0:T(8,128)S(1)}) fusion(f32[32,128]{1,0:T(8,128)S(1)} %bitcast.211, f32[32,128]{1,0:T(8,128)S(1)} %bitcast.210, f32[32,128]{1,0:T(8,128)S(1)} %bitcast.212, ...), kind=kLoop, calls=%fused_computation.62.clone.1 | loop fusion | flops 35627008 | bytes 245888 | tf_op jit(solution)/shard_map/while/body/eval_jaxpr/reduce_sum | solution.py:77
  145.8 7.5 %fusion.99 = (f32[32,128]{1,0:T(8,128)S(1)}, f32[32,128]{1,0:T(8,128)S(1)}, f32[32,128]{1,0:T(8,128)S(1)}, f32[32,128]{1,0:T(8,128)S(1)}, f32[32,128]{1,0:T(8,128)S(1)}, /*index=5*/f32[32,128]{1,0:T(8,128)S(1)}) fusion(f32[32,128]{1,0:T(8,128)S(1)} %bitcast.211, f32[32,128]{1,0:T(8,128)S(1)} %bitcast.210, f32[32,128]{1,0:T(8,128)S(1)} %bitcast.212, ...), kind=kLoop, calls=%fused_computation.62.clone.1 | loop fusion | flops 35627008 | bytes 245888 | tf_op jit(solution)/shard_map/while/body/eval_jaxpr/reduce_sum | solution.py:77
  157.4 7.5 %fusion.99 = (f32[32,128]{1,0:T(8,128)S(1)}, f32[32,128]{1,0:T(8,128)S(1)}, f32[32,128]{1,0:T(8,128)S(1)}, f32[32,128]{1,0:T(8,128)S(1)}, f32[32,128]{1,0:T(8,128)S(1)}, /*index=5*/f32[32,128]{1,0:T(8,128)S(1)}) fusion(f32[32,128]{1,0:T(8,128)S(1)} %bitcast.211, f32[32,128]{1,0:T(8,128)S(1)} %bitcast.210, f32[32,128]{1,0:T(8,128)S(1)} %bitcast.212, ...), kind=kLoop, calls=%fused_computation.62.clone.1 | loop fusion | flops 35627008 | bytes 245888 | tf_op jit(solution)/shard_map/while/body/eval_jaxpr/reduce_sum | solution.py:77
  169.0 7.5 %fusion.99 = (f32[32,128]{1,0:T(8,128)S(1)}, f32[32,128]{1,0:T(8,128)S(1)}, f32[32,128]{1,0:T(8,128)S(1)}, f32[32,128]{1,0:T(8,128)S(1)}, f32[32,128]{1,0:T(8,128)S(1)}, /*index=5*/f32[32,128]{1,0:T(8,128)S(1)}) fusion(f32[32,128]{1,0:T(8,128)S(1)} %bitcast.211, f32[32,128]{1,0:T(8,128)S(1)} %bitcast.210, f32[32,128]{1,0:T(8,128)S(1)} %bitcast.212, ...), kind=kLoop, calls=%fused_computation.62.clone.1 | loop fusion | flops 35627008 | bytes 245888 | tf_op jit(solution)/shard_map/while/body/eval_jaxpr/reduce_sum | solution.py:77
  180.6 7.5 %fusion.99 = (f32[32,128]{1,0:T(8,128)S(1)}, f32[32,128]{1,0:T(8,128)S(1)}, f32[32,128]{1,0:T(8,128)S(1)}, f32[32,128]{1,0:T(8,128)S(1)}, f32[32,128]{1,0:T(8,128)S(1)}, /*index=5*/f32[32,128]{1,0:T(8,128)S(1)}) fusion(f32[32,128]{1,0:T(8,128)S(1)} %bitcast.211, f32[32,128]{1,0:T(8,128)S(1)} %bitcast.210, f32[32,128]{1,0:T(8,128)S(1)} %bitcast.212, ...), kind=kLoop, calls=%fused_computation.62.clone.1 | loop fusion | flops 35627008 | bytes 245888 | tf_op jit(solution)/shard_map/while/body/eval_jaxpr/reduce_sum | solution.py:77
  188.4 68.3 %fusion.41 = f32[3,3,3,512]{3,0,2,1:T(4,128)S(1)} fusion(s32[4096]{0:T(1024)S(1)} %bitcast.229, s32[3,3,512]{2,1,0:T(4,128)S(1)} %multiply_add_fusion, s32[4096]{0:T(1024)S(1)} %bitcast.228, f32[1,4096]{1,0:T(1,128)S(1)} %bitcast.227, f32[1,4096]{1,0:T(1,128)S(1)} %bitcast.231, f32[1,4096]{1,0:T(1,128)S(1)} %bitcast.230), kind=kOutput, calls=%fused_computation.84 | convolution fusion | flops 773885952 | bytes 155648 | tf_op jit(solution)/shard_map/dot_general | solution.py:179
  256.7 3.2 %collective-permute-start.4 = (f32[3,3,512]{2,0,1:T(4,128)S(1)}, f32[3,3,512]{2,0,1:T(4,128)S(1)}, u32[]{:S(2)}, u32[]{:S(2)}) collective-permute-start(f32[3,3,512]{2,0,1:T(4,128)S(1)} %get-tuple-element.110), channel_id=1, source_target_pairs={{224,0},{0,32},{32,64},{64,96},{96,128},{128,160},{160,192},{192,2... | collective-permute-start | bytes 55304 | tf_op jit(solution)/shard_map/ppermute | solution.py:23
  259.9 4.4 %collective-permute-start.5 = (f32[3,3,512]{2,0,1:T(4,128)S(1)}, f32[3,3,512]{2,0,1:T(4,128)S(1)}, u32[]{:S(2)}, u32[]{:S(2)}) collective-permute-start(f32[3,3,512]{2,0,1:T(4,128)S(1)} %get-tuple-element.111), channel_id=1, source_target_pairs={{32,0},{64,32},{96,64},{128,96},{160,128},{192,160},{224,192},{0,2... | collective-permute-start | bytes 55304 | tf_op jit(solution)/shard_map/ppermute | solution.py:23
  265.2 6.5 %collective-permute-start.11 = (f32[315,8]{0,1:T(8,128)S(1)}, f32[315,8]{0,1:T(8,128)S(1)}, u32[]{:S(2)}, u32[]{:S(2)}) collective-permute-start(f32[315,8]{0,1:T(8,128)S(1)} %get-tuple-element.123), channel_id=1, source_target_pairs={{32,0},{64,32},{96,64},{128,96},{160,128},{192,160},{224,192},{0,2... | collective-permute-start | bytes 30248 | tf_op jit(solution)/shard_map/ppermute | solution.py:23
  271.9 7.6 %collective-permute-start.7 = (f32[3,512]{1,0:T(4,128)S(1)}, f32[3,512]{1,0:T(4,128)S(1)}, u32[]{:S(2)}, u32[]{:S(2)}) collective-permute-start(f32[3,512]{1,0:T(4,128)S(1)} %get-tuple-element.127), channel_id=1, source_target_pairs={{1,0},{2,1},{3,2},{4,3},{5,4},{6,5},{7,6},{8,7},{9,8},{10,9},{11,1... | collective-permute-start | bytes 18440 | tf_op jit(solution)/shard_map/ppermute | solution.py:23
  (277 shorter events, 44.8 us)
Async XLA Ops:
  0.6 16.9 %copy-start.1 = (s32[35]{0:T(128)S(1)}, s32[35]{0:T(128)}, u32[]{:S(2)}) copy-start(s32[35]{0:T(128)} %constant.159) | copy-start | bytes 424
  0.6 16.9 %copy-start = (f32[1,1,3,4096]{3,1,2,0:T(1,128)S(1)}, f32[1,1,3,4096]{3,1,2,0:T(1,128)}, u32[]{:S(2)}) copy-start(f32[1,1,3,4096]{3,1,2,0:T(1,128)} %param.25) | copy-start | bytes 147460
  3.9 37.9 %collective-permute-start = (f32[3,2,9,128]{3,2,1,0:T(8,128)S(1)}, f32[3,2,9,128]{3,2,1,0:T(8,128)S(1)}, u32[]{:S(2)}, u32[]{:S(2)}) collective-permute-start(f32[3,2,9,128]{3,2,1,0:T(8,128)S(1)} %get-tuple-element.106), channel_id=1, source_target_pairs={{224,0},{0,32},{32,64},{64,96},{96,128},{128,160},{160,192},{192,2... | collective-permute-start | bytes 82952 | tf_op jit(solution)/shard_map/ppermute | solution.py:23
  11.7 30.2 %collective-permute-start.1 = (f32[3,2,9,128]{3,2,1,0:T(8,128)S(1)}, f32[3,2,9,128]{3,2,1,0:T(8,128)S(1)}, u32[]{:S(2)}, u32[]{:S(2)}) collective-permute-start(f32[3,2,9,128]{3,2,1,0:T(8,128)S(1)} %get-tuple-element.107), channel_id=1, source_target_pairs={{32,0},{64,32},{96,64},{128,96},{160,128},{192,160},{224,192},{0,2... | collective-permute-start | bytes 82952 | tf_op jit(solution)/shard_map/ppermute | solution.py:23
  34.5 7.3 %copy-start.7 = (s32[1,1,32,12]{2,1,3,0:T(1,128)S(1)}, s32[1,1,32,12]{2,1,3,0:T(1,128)}, u32[]{:S(2)}) copy-start(s32[1,1,32,12]{2,1,3,0:T(1,128)} %param.32) | copy-start | bytes 4612
  34.5 13.5 %copy-start.15 = (f32[9]{0:T(128)S(1)}, f32[9]{0:T(128)}, u32[]{:S(2)}) copy-start(f32[9]{0:T(128)} %constant.84.clone) | copy-start | bytes 112
  34.5 13.6 %copy-start.14 = (f32[9]{0:T(128)S(1)}, f32[9]{0:T(128)}, u32[]{:S(2)}) copy-start(f32[9]{0:T(128)} %constant.85.clone) | copy-start | bytes 112
  34.5 13.9 %copy-start.13 = (f32[9]{0:T(128)S(1)}, f32[9]{0:T(128)}, u32[]{:S(2)}) copy-start(f32[9]{0:T(128)} %constant.86.clone) | copy-start | bytes 112
  34.6 14.0 %copy-start.12 = (f32[9]{0:T(128)S(1)}, f32[9]{0:T(128)}, u32[]{:S(2)}) copy-start(f32[9]{0:T(128)} %constant.87.clone) | copy-start | bytes 112
  34.6 14.0 %copy-start.11 = (f32[9]{0:T(128)S(1)}, f32[9]{0:T(128)}, u32[]{:S(2)}) copy-start(f32[9]{0:T(128)} %constant.88.clone) | copy-start | bytes 112
  34.6 14.1 %copy-start.10 = (f32[9]{0:T(128)S(1)}, f32[9]{0:T(128)}, u32[]{:S(2)}) copy-start(f32[9]{0:T(128)} %constant.89.clone) | copy-start | bytes 112
  34.6 14.2 %copy-start.9 = (f32[9]{0:T(128)S(1)}, f32[9]{0:T(128)}, u32[]{:S(2)}) copy-start(f32[9]{0:T(128)} %constant.90.clone) | copy-start | bytes 112
  34.6 14.2 %copy-start.8 = (f32[9]{0:T(128)S(1)}, f32[9]{0:T(128)}, u32[]{:S(2)}) copy-start(f32[9]{0:T(128)} %constant.91.clone) | copy-start | bytes 112
  34.6 14.3 %copy-start.17 = (s32[1,1,32]{2,1,0:T(1,128)S(1)}, s32[1,1,32]{2,1,0:T(1,128)}, u32[]{:S(2)}) copy-start(s32[1,1,32]{2,1,0:T(1,128)} %param.33) | copy-start | bytes 388
  39.9 7.6 %collective-permute-start.8 = (f32[315,3,8]{0,2,1:T(8,128)S(1)}, f32[315,3,8]{0,2,1:T(8,128)S(1)}, u32[]{:S(2)}, u32[]{:S(2)}) collective-permute-start(f32[315,3,8]{0,2,1:T(8,128)S(1)} %get-tuple-element.108), channel_id=1, source_target_pairs={{31,0},{0,1},{1,2},{2,3},{3,4},{4,5},{5,6},{6,7},{7,8},{8,9},{9,10... | collective-permute-start | bytes 90728 | tf_op jit(solution)/shard_map/ppermute | solution.py:23
  41.6 6.0 %collective-permute-start.9 = (f32[315,3,8]{0,2,1:T(8,128)S(1)}, f32[315,3,8]{0,2,1:T(8,128)S(1)}, u32[]{:S(2)}, u32[]{:S(2)}) collective-permute-start(f32[315,3,8]{0,2,1:T(8,128)S(1)} %get-tuple-element.109), channel_id=1, source_target_pairs={{1,0},{2,1},{3,2},{4,3},{5,4},{6,5},{7,6},{8,7},{9,8},{10,9},{11,1... | collective-permute-start | bytes 90728 | tf_op jit(solution)/shard_map/ppermute | solution.py:23
  41.9 6.1 %collective-permute-start.2 = (f32[3,2,9,128]{3,2,1,0:T(8,128)S(1)}, f32[3,2,9,128]{3,2,1,0:T(8,128)S(1)}, u32[]{:S(2)}, u32[]{:S(2)}) collective-permute-start(f32[3,2,9,128]{3,2,1,0:T(8,128)S(1)} %pad_maximum_fusion.1), channel_id=1, source_target_pairs={{31,0},{0,1},{1,2},{2,3},{3,4},{4,5},{5,6},{6,7},{7,8},{8,9},{9,10... | collective-permute-start | bytes 82952 | tf_op jit(solution)/shard_map/ppermute | solution.py:23
  43.7 4.7 %collective-permute-start.3 = (f32[3,2,9,128]{3,2,1,0:T(8,128)S(1)}, f32[3,2,9,128]{3,2,1,0:T(8,128)S(1)}, u32[]{:S(2)}, u32[]{:S(2)}) collective-permute-start(f32[3,2,9,128]{3,2,1,0:T(8,128)S(1)} %pad_maximum_fusion.2), channel_id=1, source_target_pairs={{1,0},{2,1},{3,2},{4,3},{5,4},{6,5},{7,6},{8,7},{9,8},{10,9},{11,1... | collective-permute-start | bytes 82952 | tf_op jit(solution)/shard_map/ppermute | solution.py:23
  256.7 15.1 %collective-permute-start.4 = (f32[3,3,512]{2,0,1:T(4,128)S(1)}, f32[3,3,512]{2,0,1:T(4,128)S(1)}, u32[]{:S(2)}, u32[]{:S(2)}) collective-permute-start(f32[3,3,512]{2,0,1:T(4,128)S(1)} %get-tuple-element.110), channel_id=1, source_target_pairs={{224,0},{0,32},{32,64},{64,96},{96,128},{128,160},{160,192},{192,2... | collective-permute-start | bytes 55304 | tf_op jit(solution)/shard_map/ppermute | solution.py:23
  259.9 11.9 %collective-permute-start.5 = (f32[3,3,512]{2,0,1:T(4,128)S(1)}, f32[3,3,512]{2,0,1:T(4,128)S(1)}, u32[]{:S(2)}, u32[]{:S(2)}) collective-permute-start(f32[3,3,512]{2,0,1:T(4,128)S(1)} %get-tuple-element.111), channel_id=1, source_target_pairs={{32,0},{64,32},{96,64},{128,96},{160,128},{192,160},{224,192},{0,2... | collective-permute-start | bytes 55304 | tf_op jit(solution)/shard_map/ppermute | solution.py:23
  264.3 15.2 %collective-permute-start.10 = (f32[315,8]{0,1:T(8,128)S(1)}, f32[315,8]{0,1:T(8,128)S(1)}, u32[]{:S(2)}, u32[]{:S(2)}) collective-permute-start(f32[315,8]{0,1:T(8,128)S(1)} %get-tuple-element.122), channel_id=1, source_target_pairs={{224,0},{0,32},{32,64},{64,96},{96,128},{128,160},{160,192},{192,2... | collective-permute-start | bytes 30248 | tf_op jit(solution)/shard_map/ppermute | solution.py:23
  265.2 14.2 %collective-permute-start.11 = (f32[315,8]{0,1:T(8,128)S(1)}, f32[315,8]{0,1:T(8,128)S(1)}, u32[]{:S(2)}, u32[]{:S(2)}) collective-permute-start(f32[315,8]{0,1:T(8,128)S(1)} %get-tuple-element.123), channel_id=1, source_target_pairs={{32,0},{64,32},{96,64},{128,96},{160,128},{192,160},{224,192},{0,2... | collective-permute-start | bytes 30248 | tf_op jit(solution)/shard_map/ppermute | solution.py:23
  271.8 8.3 %collective-permute-start.6 = (f32[3,512]{1,0:T(4,128)S(1)}, f32[3,512]{1,0:T(4,128)S(1)}, u32[]{:S(2)}, u32[]{:S(2)}) collective-permute-start(f32[3,512]{1,0:T(4,128)S(1)} %get-tuple-element.126), channel_id=1, source_target_pairs={{31,0},{0,1},{1,2},{2,3},{3,4},{4,5},{5,6},{6,7},{7,8},{8,9},{9,10... | collective-permute-start | bytes 18440 | tf_op jit(solution)/shard_map/ppermute | solution.py:23
  271.9 8.4 %collective-permute-start.7 = (f32[3,512]{1,0:T(4,128)S(1)}, f32[3,512]{1,0:T(4,128)S(1)}, u32[]{:S(2)}, u32[]{:S(2)}) collective-permute-start(f32[3,512]{1,0:T(4,128)S(1)} %get-tuple-element.127), channel_id=1, source_target_pairs={{1,0},{2,1},{3,2},{4,3},{5,4},{6,5},{7,6},{8,7},{9,8},{10,9},{11,1... | collective-permute-start | bytes 18440 | tf_op jit(solution)/shard_map/ppermute | solution.py:23
  (6 other events, 33.1 us)
where the time goes:
time: 286 us; the launch traced here: 281 us
  other arithmetic  110 us (38%)
  matrix products  73.6 us (26%)
  starting transfers between devices  40.2 us (14%)
  local copies, waits for them, and re-layouts  30.5 us (11%)
  loops' own time  24.9 us (9%)
    reduce_sum x12, other arithmetic, pair_stress(): entries.append(jnp.sum(weight * entry_value, axis=2))  90.5 us
    dot_general x1, matrix products, on_device(): jnp.dot(0.5 * force, incidence, precision=highest, preferred_element_type...  68.3 us
    ppermute x12, starting transfers between devices, passed_along(): return lax.ppermute(block, axis, route)  40.2 us
    another operation x1, loops' own time, on_device(): lax.scan(add_slot, jnp.zeros((6, own_count, TILE), jnp.float32), jnp.aran...  24.9 us
    mul x12, other arithmetic, pair_stress(): weight = shear_scale * valid_weight[:, None, None] * inverse / radius_sq  7.8 us
    mul x1, local copies, waits for them, and re-layouts, moment_terms(): products[:, None, :] * monomial[None, :, :]  7.28 us
    dynamic_slice x12, local copies, waits for them, and re-layouts, on_device(): lax.scan(add_slot, jnp.zeros((6, own_count, TILE), jnp.float32), jnp.aran...  7.04 us
    gather x12, local copies, waits for them, and re-layouts, add_slot(): source_tiles = source_pool[pair_rows[:, slot_index]].transpose(1, 0, 2)  7.02 us
  transfers between devices with their start and end apart: 12, of which 3 were waited for; matrix products, arithmetic and copies ran while one was open for 9% of the time, Pallas kernels for 0%

commit v1 on v0

v1 whole, which is shorter than its diff:
```python
import jax
import jax.numpy as jnp
from jax import lax
from jax.experimental import pallas as pl
from jax.experimental.pallas import tpu as pltpu
from jax.sharding import PartitionSpec as P

TILE = 128
TILES = 32
GHOST = 2
NP = 12
NODE_DEV = 512
CELL_DEV = 8
COMPONENTS = 315
POOL = 48
FEATURES = 40
AUG = 32
TERMS = 368

core_radius = 0.1
shear_scale = 0.25
neighbour_offsets = ((-1, -1), (-1, 0), (-1, 1), (0, -1), (0, 1), (1, -1), (1, 0), (1, 1))
f32 = jnp.float32
bf16 = jnp.bfloat16
MESH = pl.DeviceIdType.MESH
NT = (((1,), (1,)), ((), ()))


def rounded(value):
    return value.astype(bf16).astype(f32)


def pieces(value, count):
    parts = []
    for _ in range(count - 1):
        part = rounded(value)
        parts.append(part)
        value = value - part
    parts.append(rounded(value))
    return parts


def exponent_table():
    exponent_rows = []
    for degree in range(5):
        for first_power in range(degree, -1, -1):
            for second in range(degree - first_power, -1, -1):
                exponent_rows.append((first_power, second, degree - first_power - second))
    return exponent_rows


def cross(u, v):
    return [
        u[1] * v[2] - u[2] * v[1],
        u[2] * v[0] - u[0] * v[2],
        u[0] * v[1] - u[1] * v[0],
    ]


def dot3(u, v):
    return u[0] * v[0] + u[1] * v[1] + u[2] * v[2]


PAIRS6 = ((0, 0), (1, 1), (2, 2), (0, 1), (0, 2), (1, 2))
SYM = {}
for _slot, (_m, _n) in enumerate(PAIRS6):
    SYM[(_m, _n)] = _slot
    SYM[(_n, _m)] = _slot


def source_features(y, line, burgers):
    g = [shear_scale * v for v in cross(burgers, line)]
    h = [[y[k] * g[n] for n in range(3)] for k in range(3)]
    q = [[y[k] * h[l][n] for n in range(3)] for (k, l) in PAIRS6]
    y2 = dot3(y, y)
    trace = h[0][0] + h[1][1] + h[2][2]
    c = []
    for m, n in PAIRS6:
        value = y2 * (h[m][n] + h[n][m]) - 3.0 * trace * (y[m] * y[n])
        if m == n:
            value = value + y2 * trace
        c.append(value)
    rows = list(g)
    for k in range(3):
        rows += h[k]
    for kl in range(6):
        rows += q[kl]
    rows += c
    return rows


def stress_from_moments(x, moment):
    c2 = core_radius**2
    G = moment[0:3]
    H = [moment[3 + 3 * k : 6 + 3 * k] for k in range(3)]
    Q = [moment[12 + 3 * kl : 15 + 3 * kl] for kl in range(6)]
    C = moment[30:36]
    x2 = dot3(x, x)
    xG = dot3(x, G)
    trH = H[0][0] + H[1][1] + H[2][2]
    Z = [Q[0][n] + Q[1][n] + Q[2][n] for n in range(3)]
    W = [Q[SYM[(0, n)]][0] + Q[SYM[(1, n)]][1] + Q[SYM[(2, n)]][2] for n in range(3)]
    xH = [x[0] * H[0][n] + x[1] * H[1][n] + x[2] * H[2][n] for n in range(3)]
    Hx = [H[n][0] * x[0] + H[n][1] * x[1] + H[n][2] * x[2] for n in range(3)]
    xQ = [
        [x[0] * Q[SYM[(0, m)]][n] + x[1] * Q[SYM[(1, m)]][n] + x[2] * Q[SYM[(2, m)]][n] for n in range(3)]
        for m in range(3)
    ]
    lead = [(x2 + c2) * G[n] - 2.0 * xH[n] + Z[n] + 3.0 * Hx[n] - 3.0 * W[n] for n in range(3)]
    both = xG - trH
    diagonal = (
        (x2 + 2.5 * c2) * both
        - 2.0 * dot3(x, xH)
        + 2.0 * dot3(x, W)
        + dot3(x, Z)
    )
    out = []
    for m, n in PAIRS6:
        value = (
            x[m] * lead[n]
            + x[n] * lead[m]
            - (x2 + c2) * (H[m][n] + H[n][m])
            + 2.0 * (xQ[m][n] + xQ[n][m])
            - 3.0 * (x[m] * x[n] * both + dot3(x, Q[SYM[(m, n)]]))
            - C[SYM[(m, n)]]
        )
        if m == n:
            value = value + diagonal
        out.append(value)
    return out


PIECE_X = (0, 0, 1, 1, 0, 2)
PIECE_Y = (0, 1, 0, 1, 2, 0)


def field_rows(x):
    one = jnp.ones_like(x[0])
    rows = []
    for c in range(3):
        part = pieces(x[c], 3)
        rows += [part[j] for j in PIECE_X]
    rows += pieces(dot3(x, x) + core_radius**2, 3)
    rows += [one, one, one]
    return rows


def source_rows(y):
    one = jnp.ones_like(y[0])
    rows = []
    for c in range(3):
        part = pieces(-2.0 * y[c], 3)
        rows += [part[j] for j in PIECE_Y]
    rows += [one, one, one]
    rows += pieces(dot3(y, y), 3)
    return rows


def kernel(
    mid_ref, line_ref, burg_ref, cell_ref, node_ref, glist, gcount, plist, pcount,
    nout_ref, cout_ref,
    S, own, pkt, ghost, feat, FT, yrow, YT, xrow, XB, R2, VS, MT, mono, bl, cacc, cpkt, crecv,
    frow, nacc, npkt, nrecv, send_sem, recv_sem,
):
    i = lax.axis_index("dx")
    j = lax.axis_index("dy")
    ndx = lax.axis_size("dx")
    ndy = lax.axis_size("dy")
    peers = [
        (lax.rem(i + (a + ndx), ndx), lax.rem(j + (b + ndy), ndy)) for a, b in neighbour_offsets
    ]

    barrier = pltpu.get_barrier_semaphore()
    for peer in peers:
        pl.semaphore_signal(barrier, inc=1, device_id=peer, device_id_type=MESH)

    def sends(kind, source, target):
        copies = []
        for k in range(8):
            copies.append(
                pltpu.make_async_remote_copy(
                    src_ref=source(k),
                    dst_ref=target.at[7 - k],
                    send_sem=send_sem.at[kind, k],
                    recv_sem=recv_sem.at[kind, 7 - k],
                    device_id=peers[k],
                    device_id_type=MESH,
                )
            )
        return copies

    for t in range(TILES):
        window = pl.ds(t * TILE, TILE)
        for first, ref in ((0, mid_ref), (3, line_ref), (6, burg_ref)):
            values = ref[0, 0, :, window]
            S[first : first + 3, t, :] = values
            own[t, first : first + 3, :] = values
    for k in range(8):
        for g in range(GHOST):
            valid = jnp.minimum(jnp.maximum(gcount[0, 0, k] - g, 0), 1).astype(f32)
            pkt[k, :, g, :] = own[glist[0, 0, k, g]] * valid

    ghost_copies = sends(0, lambda k: pkt.at[k], ghost)
    zero_rows = jnp.zeros((AUG, TILE), f32)

    def prepare_sources(first, count):
        rows = pl.ds(first, count)
        y = [S[c, rows, :] - 0.5 for c in range(3)]
        line = [S[3 + c, rows, :] for c in range(3)]
        burgers = [S[6 + c, rows, :] for c in range(3)]
        for index, value in enumerate(source_features(y, line, burgers)):
            feat[rows, index, :] = value
        for index, value in enumerate(source_rows(y)):
            yrow[rows, index, :] = value
        zero = jnp.zeros_like(y[0])
        for index in range(36, FEATURES):
            feat[rows, index, :] = zero
        for index in range(24, AUG):
            yrow[rows, index, :] = zero

        def per_tile(t, carry):
            FT[t] = jnp.concatenate(pieces(feat[t], 3), axis=0).astype(bf16)
            rows_t = yrow[t]
            YT[0, t] = jnp.concatenate([rows_t, zero_rows], axis=0).T.astype(bf16)
            YT[1, t] = jnp.concatenate([zero_rows, rows_t], axis=0).T.astype(bf16)
            return carry

        lax.fori_loop(first, first + count, per_tile, 0, unroll=4)

    prepare_sources(0, TILES)

    own_x = [S[c, 0:TILES, :] - 0.5 for c in range(3)]
    field = field_rows(own_x)
    for index, value in enumerate(field):
        xrow[:, index, :] = value
    for index in range(len(field), AUG):
        xrow[:, index, :] = jnp.zeros((TILES, TILE), f32)

    def field_tile(t, carry):
        rows_t = xrow[t]
        left = jnp.concatenate([rows_t, zero_rows], axis=0)
        right = jnp.concatenate([zero_rows, rows_t], axis=0)
        XB[t] = jnp.concatenate([left, right], axis=1).astype(bf16)
        return carry

    lax.fori_loop(0, TILES, field_tile, 0, unroll=4)
    FT[POOL] = jnp.zeros((3 * FEATURES, TILE), bf16)

    pl.semaphore_wait(barrier, 8)
    for copy in ghost_copies:
        copy.start()

    scaled = [2.0 * (S[c, 0:TILES, :] - 0.5) for c in range(3)]
    powers = []
    for u in scaled:
        square = u * u
        powers.append([jnp.ones_like(u), u, square, square * u, square * square])
    for r, (e0, e1, e2) in enumerate(exponent_table()):
        mono[:, r, :] = powers[0][e0] * powers[1][e1] * powers[2][e2]
    for r in range(35, 40):
        mono[:, r, :] = jnp.zeros((TILES, TILE), f32)
    for beta in range(3):
        for gamma in range(3):
            bl[:, 3 * beta + gamma, :] = S[6 + beta, 0:TILES, :] * S[3 + gamma, 0:TILES, :]
    cacc[...] = jnp.zeros_like(cacc)
    sub128 = lax.broadcasted_iota(jnp.int32, (TILE, TILE), 0)

    def cell_group(group, carry):
        highs, lows, members = [], [], []
        for inner in range(4):
            t = group * 4 + inner
            mono_t = mono[t]
            bl_t = bl[t]
            block = [bl_t[k : k + 1, :] * mono_t for k in range(9)]
            block.append(jnp.zeros((8, TILE), f32))
            terms = jnp.concatenate(block, axis=0)
            high = terms.astype(bf16)
            highs.append(high)
            lows.append((terms - high.astype(f32)).astype(bf16))
            cells = cell_ref[0, :, pl.ds(pl.multiple_of(t * TILE, TILE), TILE)]
            members.append(jnp.where(sub128 == cells, 1.0, 0.0).astype(bf16))
        lhs = jnp.concatenate(
            [jnp.concatenate(highs, axis=1), jnp.concatenate(lows, axis=1)], axis=0
        )
        rhs = jnp.concatenate(members, axis=1)
        cacc[...] += lax.dot_general(lhs, rhs, NT, preferred_element_type=f32)
        return carry

    lax.fori_loop(0, TILES // 4, cell_group, 0)
    for block in range(3):
        rows = min(TILE, TERMS - block * TILE)
        part = cacc[block * TILE : block * TILE + rows, :] + cacc[TERMS + block * TILE : TERMS + block * TILE + rows, :]
        if rows < TILE:
            part = jnp.concatenate([part, jnp.zeros((TILE - rows, TILE), f32)], axis=0)
        turned = part.T
        for d in range(9):
            cpkt[d, :, block * TILE : (block + 1) * TILE] = turned[8 * d : 8 * d + 8, :]
    cell_copies = sends(1, lambda k: cpkt.at[k + (k >= 4)], crecv)
    for copy in cell_copies:
        copy.start()

    for k in range(8):
        ghost_copies[k].wait()
    for q in range(8):
        a, b = neighbour_offsets[q]
        rows = pl.ds(TILES + GHOST * q, GHOST)
        S[0, rows, :] = ghost[q, 0] + float(a)
        S[1, rows, :] = ghost[q, 1] + float(b)
        for c in range(2, 9):
            S[c, rows, :] = ghost[q, c]
    prepare_sources(TILES, POOL - TILES)

    def stage_inner(t):
        rhs = XB[t]
        for pair in range(NP // 2):
            lhs = YT[0, plist[0, 0, t, 2 * pair]] + YT[1, plist[0, 0, t, 2 * pair + 1]]
            R2[pair] = jnp.dot(lhs, rhs, preferred_element_type=f32)

    def stage_power():
        for n in range(NP):
            radius_sq = R2[n // 2, :, (n % 2) * TILE : (n % 2 + 1) * TILE]
            inverse = lax.rsqrt(radius_sq)
            square = inverse * inverse
            value = square * square * inverse
            high = value.astype(bf16)
            VS[n * TILE : (n + 1) * TILE, 0:TILE] = high
            VS[n * TILE : (n + 1) * TILE, TILE : 2 * TILE] = (value - high.astype(f32)).astype(bf16)

    def stage_sum(t):
        count = pcount[0, 0, t]
        chosen = []
        for n in range(NP):
            valid = jnp.minimum(jnp.maximum(count - n, 0), 1)
            chosen.append(FT[valid * (plist[0, 0, t, n] - POOL) + POOL])
        total = jnp.dot(jnp.concatenate(chosen, axis=1), VS[...], preferred_element_type=f32)
        total = total[:, 0:TILE] + total[:, TILE : 2 * TILE]
        MT[t] = total[0:FEATURES] + total[FEATURES : 2 * FEATURES] + total[2 * FEATURES : 3 * FEATURES]

    stage_inner(0)
    stage_power()
    stage_inner(1)

    def pair_step(t, carry):
        stage_sum(t - 2)
        stage_power()
        stage_inner(t)
        return carry

    lax.fori_loop(2, TILES, pair_step, 0)
    stage_sum(TILES - 2)
    stage_power()
    stage_sum(TILES - 1)

    x = [S[c, 0:TILES, :] - 0.5 for c in range(3)]
    stress = stress_from_moments(x, [MT[:, r, :] for r in range(36)])
    burgers = [S[6 + c, 0:TILES, :] for c in range(3)]
    line = [S[3 + c, 0:TILES, :] for c in range(3)]
    traction = [dot3([stress[SYM[(m, n)]] for n in range(3)], burgers) for m in range(3)]
    force = cross(traction, line)
    for c in range(3):
        for piece, value in enumerate(pieces(0.5 * force[c], 2)):
            frow[:, 2 * c + piece, :] = value
    nacc[...] = jnp.zeros_like(nacc)
    sub40 = lax.broadcasted_iota(jnp.int32, (40, TILE), 0)

    def node_group(group, carry):
        lefts, rights = [], []
        for inner in range(4):
            t = group * 4 + inner
            rows_t = frow[t]
            for end in range(2):
                nodes = node_ref[0, 0, end : end + 1, pl.ds(pl.multiple_of(t * TILE, TILE), TILE)]
                outer = sub40 == lax.shift_right_logical(nodes, 7)
                lefts.append(
                    jnp.concatenate(
                        [jnp.where(outer, rows_t[r : r + 1, :], 0.0) for r in range(6)], axis=0
                    ).astype(bf16)
                )
                rights.append(jnp.where(sub128 == (nodes & 127), 1.0, 0.0).astype(bf16))
        nacc[...] += lax.dot_general(
            jnp.concatenate(lefts, axis=1),
            jnp.concatenate(rights, axis=1),
            NT,
            preferred_element_type=f32,
        )
        return carry

    lax.fori_loop(0, TILES // 4, node_group, 0)
    for c in range(3):
        total = nacc[80 * c : 80 * c + 40, :] + nacc[80 * c + 40 : 80 * c + 80, :]
        for d in range(9):
            npkt[d, c] = total[4 * d : 4 * d + 4, :]
    node_copies = sends(2, lambda k: npkt.at[k + (k >= 4)], nrecv)
    for copy in node_copies:
        copy.start()

    for copy in cell_copies:
        copy.wait()
    moments = cpkt[4]
    for q in range(8):
        moments = moments + crecv[q]
    turned = []
    for block in range(3):
        part = moments[:, block * TILE : (block + 1) * TILE]
        part = jnp.concatenate([part, jnp.zeros((TILE - CELL_DEV, TILE), f32)], axis=0)
        turned.append(part.T)
    turned = jnp.concatenate(turned, axis=0)
    for k in range(9):
        cout_ref[35 * k : 35 * k + 35, :] = turned[40 * k : 40 * k + 35, 0:CELL_DEV]
    for copy in node_copies:
        copy.wait()
    nodes = npkt[4]
    for q in range(8):
        nodes = nodes + nrecv[q]
    for quarter in range(4):
        nout_ref[0, 0, :, quarter * TILE : (quarter + 1) * TILE] = nodes[:, quarter, :]


def on_device(*arguments):
    vmem = pl.BlockSpec(memory_space=pltpu.VMEM)
    smem = pl.BlockSpec(memory_space=pltpu.SMEM)
    return pl.pallas_call(
        kernel,
        out_shape=(
            jax.ShapeDtypeStruct((1, 1, 3, NODE_DEV), f32),
            jax.ShapeDtypeStruct((COMPONENTS, CELL_DEV), f32),
        ),
        in_specs=[vmem] * 5 + [smem] * 4,
        out_specs=(vmem, vmem),
        scratch_shapes=[
            pltpu.VMEM((9, POOL, TILE), f32),
            pltpu.VMEM((TILES, 9, TILE), f32),
            pltpu.VMEM((8, 9, GHOST, TILE), f32),
            pltpu.VMEM((8, 9, GHOST, TILE), f32),
            pltpu.VMEM((POOL, FEATURES, TILE), f32),
            pltpu.VMEM((POOL + 1, 3 * FEATURES, TILE), bf16),
            pltpu.VMEM((POOL, AUG, TILE), f32),
            pltpu.VMEM((2, POOL, TILE, 2 * AUG), bf16),
            pltpu.VMEM((TILES, AUG, TILE), f32),
            pltpu.VMEM((TILES, 2 * AUG, 2 * TILE), bf16),
            pltpu.VMEM((NP // 2, TILE, 2 * TILE), f32),
            pltpu.VMEM((NP * TILE, 2 * TILE), bf16),
            pltpu.VMEM((TILES, FEATURES, TILE), f32),
            pltpu.VMEM((TILES, 40, TILE), f32),
            pltpu.VMEM((TILES, 16, TILE), f32),
            pltpu.VMEM((2 * TERMS, TILE), f32),
            pltpu.VMEM((9, CELL_DEV, 384), f32),
            pltpu.VMEM((8, CELL_DEV, 384), f32),
            pltpu.VMEM((TILES, 8, TILE), f32),
            pltpu.VMEM((240, TILE), f32),
            pltpu.VMEM((9, 3, 4, TILE), f32),
            pltpu.VMEM((8, 3, 4, TILE), f32),
            pltpu.SemaphoreType.DMA((3, 8)),
            pltpu.SemaphoreType.DMA((3, 8)),
        ],
        compiler_params=pltpu.CompilerParams(collective_id=0, has_side_effects=True, vmem_limit_bytes=48 * 1024 * 1024),
        name="segments",
    )(*arguments)


def solution(mesh):
    in_specs = (
        P("dx", "dy", None, None),
        P("dx", "dy", None, None),
        P("dx", "dy", None, None),
        P("dx", "dy", None),
        P("dx", "dy", None, None),
        P("dx", "dy", None, None),
        P("dx", "dy", None),
        P("dx", "dy", None, None),
        P("dx", "dy", None),
    )
    out_specs = (P("dx", "dy", None, None), P(None, ("dx", "dy")))
    return jax.shard_map(
        on_device, mesh=mesh, in_specs=in_specs, out_specs=out_specs, check_vma=False
    )
```

time: 286 us -> 47.1 us (0.16); the launches traced: 281 us -> 46.8 us
  other arithmetic: 110 us -> 0 us
  matrix products: 73.6 us -> 0 us
  Pallas kernels: 0 us -> 40.9 us
  starting transfers between devices: 40.2 us -> 0 us
  local copies, waits for them, and re-layouts: 30.5 us -> 5.21 us
  loops' own time: 24.9 us -> 0 us
    reduce_sum x12 -> x0, other arithmetic: 90.5 us -> none  [pair_stress(): entries.append(jnp.sum(weight * entry_value, axis=2))]
    dot_general x2 -> x0, matrix products: 73.6 us -> none  [the longest x1 68.3 us: on_device(): jnp.dot(0.5 * force, incidence, precision=highest, preferred_element_type...]
    pallas_call x0 -> x1, Pallas kernels: none -> 40.9 us  [on_device(): pl.pallas_call(kernel, out_shape=(jax.ShapeDtypeStruct((1, 1, 3, NODE_DEV...]
    ppermute x12 -> x0, starting transfers between devices: 40.2 us -> none  [passed_along(): return lax.ppermute(block, axis, route)]
    another operation x1 -> x0, loops' own time: 24.9 us -> none  [on_device(): lax.scan(add_slot, jnp.zeros((6, own_count, TILE), jnp.float32), jnp.aran...]
    gather x16 -> x0, local copies, waits for them, and re-layouts: 13.7 us -> none  [the longest x12 7.02 us: add_slot(): source_tiles = source_pool[pair_rows[:, slot_index]].transpose(1, 0, 2)]
    mul x16 -> x0, other arithmetic: 11.3 us -> none  [the longest x12 7.8 us: pair_stress(): weight = shear_scale * valid_weight[:, None, None] * inverse / radius_sq]
    mul x2 -> x0, local copies, waits for them, and re-layouts: 7.36 us -> none  [the longest x1 7.28 us: moment_terms(): products[:, None, :] * monomial[None, :, :]]
  transfers between devices with their start and end apart: 12 -> 0, of which waited for: 3 -> 0; matrix products, arithmetic and copies ran while one was open for 9% -> 0% of each run, Pallas kernels for 0% -> 0%
where the time goes in v1:
time: 47.1 us; the launch traced here: 46.8 us
  Pallas kernels  40.9 us (87%)
  local copies, waits for them, and re-layouts  5.21 us (11%)
  between operations  0.68 us (1%)
    pallas_call x1, Pallas kernels, on_device(): pl.pallas_call(kernel, out_shape=(jax.ShapeDtypeStruct((1, 1, 3, NODE_DEV...  40.9 us
    unnamed x17, local copies, waits for them, and re-layouts  3.91 us
    pallas_call x2, local copies, waits for them, and re-layouts, on_device(): pl.pallas_call(kernel, out_shape=(jax.ShapeDtypeStruct((1, 1, 3, NODE_DEV...  1.3 us

profile of v1, /device:TPU:1, one launch (start us, length us, event | category | flops | bytes accessed | tf_op | source)
XLA Modules:
  0.0 46.8 jit_solution(12536151034718781578)
XLA Ops:
  0.6 0.8 %copy.14.glist = s32[1,1,8,2]{3,2,1,0:T(8,128)S(1)} copy(s32[1,1,8,2]{2,3,1,0:T(2,128)} %param.14) | data formatting | bytes 128 | tf_op args[5]
  1.4 0.8 %copy.15.plist = s32[1,1,32,12]{3,2,1,0:T(8,128)S(1)} copy(s32[1,1,32,12]{2,1,3,0:T(1,128)} %param.16) | data formatting | bytes 3072 | tf_op args[7]
  2.2 0.0 copy-start.4
  2.2 0.8 %copy.11.mid_ref = f32[1,1,3,4096]{3,2,1,0:T(4,128)S(1)} copy(f32[1,1,3,4096]{3,1,2,0:T(1,128)} %param.9) | data formatting | bytes 98304 | tf_op args[0]
  3.0 0.0 copy-done.4
  3.0 0.0 copy-start.5
  3.1 0.7 %copy-done.5 = f32[1,1,3,4096]{3,1,2,0:T(1,128)S(1)} copy-done((f32[1,1,3,4096]{3,1,2,0:T(1,128)S(1)}, f32[1,1,3,4096]{3,1,2,0:T(1,128)}, u32[]{:S(2)}) %copy-start.5) | copy-done | bytes 49176
  3.8 0.0 copy-start
  3.8 0.0 copy-start.1
  3.8 0.0 copy-start.2
  3.8 0.0 copy-start.3
  3.9 0.7 %copy-done = s32[1,1,2,4096]{3,2,1,0:T(2,128)S(1)} copy-done((s32[1,1,2,4096]{3,2,1,0:T(2,128)S(1)}, s32[1,1,2,4096]{3,2,1,0:T(2,128)}, u32[]{:S(2)}) %copy-start) | copy-done | bytes 32792
  4.6 0.0 copy-done.1
  4.6 0.0 copy-done.2
  4.6 0.0 copy-done.3
  4.6 40.9 %segments.1 = (f32[1,1,3,512]{3,2,1,0:T(4,128)S(1)}, f32[315,8]{1,0:T(8,128)S(1)}) custom-call(f32[1,1,3,4096]{3,2,1,0:T(4,128)S(1)} %copy.11.mid_ref, f32[1,1,3,4096]{3,2,1,0:T(4,128)S(1)} %copy.12.line_ref, f32[1,1,3,4096]{3,2,1,0:T(4,128)S(1)} %copy.13.burg_ref, s32[1,1,4096]{2,1,0:T(1,128)S(1)} %copy-done.1, s32[1,1,2,4096]{3,2,1,0:T(2,128)S(1)} %copy-done, ...), custom_call_target="tpu_custom_call" | custom-call | tf_op jit(solution)/shard_map/segments/pallas_call | solution.py:422
  45.5 0.6 %copy.16 = f32[1,1,3,512]{3,1,2,0:T(1,128)} copy(f32[1,1,3,512]{3,2,1,0:T(4,128)S(1)} %get-tuple-element.2) | data formatting | bytes 12288 | tf_op jit(solution)/shard_map/segments/pallas_call | solution.py:422
  46.1 0.7 %copy.17 = f32[315,8]{0,1:T(8,128)} copy(f32[315,8]{1,0:T(8,128)S(1)} %get-tuple-element.3) | data formatting | bytes 20160 | tf_op jit(solution)/shard_map/segments/pallas_call | solution.py:422
  (2 shorter events, 0.1 us)
Async XLA Ops:
  2.2 0.8 %copy-start.4 = (f32[1,1,3,4096]{3,1,2,0:T(1,128)S(1)}, f32[1,1,3,4096]{3,1,2,0:T(1,128)}, u32[]{:S(2)}) copy-start(f32[1,1,3,4096]{3,1,2,0:T(1,128)} %param.10) | copy-start | bytes 147460
  3.0 0.8 %copy-start.5 = (f32[1,1,3,4096]{3,1,2,0:T(1,128)S(1)}, f32[1,1,3,4096]{3,1,2,0:T(1,128)}, u32[]{:S(2)}) copy-start(f32[1,1,3,4096]{3,1,2,0:T(1,128)} %param.11) | copy-start | bytes 147460
  3.8 0.8 %copy-start = (s32[1,1,2,4096]{3,2,1,0:T(2,128)S(1)}, s32[1,1,2,4096]{3,2,1,0:T(2,128)}, u32[]{:S(2)}) copy-start(s32[1,1,2,4096]{3,2,1,0:T(2,128)} %node_ref.1) | copy-start | bytes 98308
  3.8 0.8 %copy-start.1 = (s32[1,1,4096]{2,1,0:T(1,128)S(1)}, s32[1,1,4096]{2,1,0:T(1,128)}, u32[]{:S(2)}) copy-start(s32[1,1,4096]{2,1,0:T(1,128)} %cell_ref.1) | copy-start | bytes 49156
  3.8 0.8 %copy-start.2 = (s32[1,1,8]{2,1,0:T(1,128)S(1)}, s32[1,1,8]{2,1,0:T(1,128)}, u32[]{:S(2)}) copy-start(s32[1,1,8]{2,1,0:T(1,128)} %gcount.1) | copy-start | bytes 100
  3.8 0.8 %copy-start.3 = (s32[1,1,32]{2,1,0:T(1,128)S(1)}, s32[1,1,32]{2,1,0:T(1,128)}, u32[]{:S(2)}) copy-start(s32[1,1,32]{2,1,0:T(1,128)} %pcount.1) | copy-start | bytes 388

commit v2 on v1

--- a/solution.py
+++ b/solution.py
@@ -15,6 +15,8 @@
 POOL = 48
 FEATURES = 40
 AUG = 32
+UNROLL = 6
+NODE_GROUP = 16
 TERMS = 368
 
 core_radius = 0.1
@@ -38,6 +40,11 @@
         value = value - part
     parts.append(rounded(value))
     return parts
+
+
+def each_tile(ref, index, first=0, count=TILES):
+    blocks, pitch, lanes = ref.shape
+    return ref.reshape(blocks * pitch, lanes).at[pl.ds(first * pitch + index, count, stride=pitch), :]
 
 
 def exponent_table():
@@ -157,10 +164,11 @@
 
 
 def kernel(
-    mid_ref, line_ref, burg_ref, cell_ref, node_ref, glist, gcount, plist, pcount,
+    mid_any, line_any, burg_any, cell_any, node_any, glist_any, gcount_any, plist_any, pcount_any,
     nout_ref, cout_ref,
-    S, own, pkt, ghost, feat, FT, yrow, YT, xrow, XB, R2, VS, MT, mono, bl, cacc, cpkt, crecv,
-    frow, nacc, npkt, nrecv, send_sem, recv_sem,
+    mid, line, burg, cells_in, nodes_in, glist, gcount, plist, pcount,
+    own, pkt, ghost, far, feat, FT, yrow, YT, xrow, XL, XR, R2, VH, VL, MT, mono, bl, cacc, cpkt,
+    crecv, frow, nacc, npkt, nrecv, send_sem, recv_sem, load_sem,
 ):
     i = lax.axis_index("dx")
     j = lax.axis_index("dy")
@@ -189,79 +197,95 @@
             )
         return copies
 
-    for t in range(TILES):
-        window = pl.ds(t * TILE, TILE)
-        for first, ref in ((0, mid_ref), (3, line_ref), (6, burg_ref)):
-            values = ref[0, 0, :, window]
-            S[first : first + 3, t, :] = values
-            own[t, first : first + 3, :] = values
+    loads = [
+        pltpu.make_async_copy(source, target, load_sem.at[index])
+        for index, (source, target) in enumerate(
+            (
+                (glist_any, glist),
+                (gcount_any, gcount),
+                (mid_any, mid),
+                (line_any, line),
+                (burg_any, burg),
+                (plist_any, plist),
+                (pcount_any, pcount),
+                (cell_any, cells_in),
+                (node_any, nodes_in),
+            )
+        )
+    ]
+    for load in loads:
+        load.start()
+    for load in loads:
+        load.wait()
+
+    for c in range(3):
+        each_tile(own, c)[...] = mid[c]
+        each_tile(own, 3 + c)[...] = line[c]
+        each_tile(own, 6 + c)[...] = burg[c]
     for k in range(8):
         for g in range(GHOST):
             valid = jnp.minimum(jnp.maximum(gcount[0, 0, k] - g, 0), 1).astype(f32)
-            pkt[k, :, g, :] = own[glist[0, 0, k, g]] * valid
+            pkt[k, :, g, :] = own[glist[g, k]][0:9] * valid
 
     ghost_copies = sends(0, lambda k: pkt.at[k], ghost)
     zero_rows = jnp.zeros((AUG, TILE), f32)
 
-    def prepare_sources(first, count):
-        rows = pl.ds(first, count)
-        y = [S[c, rows, :] - 0.5 for c in range(3)]
-        line = [S[3 + c, rows, :] for c in range(3)]
-        burgers = [S[6 + c, rows, :] for c in range(3)]
-        for index, value in enumerate(source_features(y, line, burgers)):
-            feat[rows, index, :] = value
+    def prepare_sources(first, count, y, line_rows, burgers, unroll):
+        for index, value in enumerate(source_features(y, line_rows, burgers)):
+            each_tile(feat, index, first, count)[...] = value
         for index, value in enumerate(source_rows(y)):
-            yrow[rows, index, :] = value
+            each_tile(yrow, index, first, count)[...] = value
         zero = jnp.zeros_like(y[0])
         for index in range(36, FEATURES):
-            feat[rows, index, :] = zero
+            each_tile(feat, index, first, count)[...] = zero
         for index in range(24, AUG):
-            yrow[rows, index, :] = zero
+            each_tile(yrow, index, first, count)[...] = zero
 
         def per_tile(t, carry):
             FT[t] = jnp.concatenate(pieces(feat[t], 3), axis=0).astype(bf16)
             rows_t = yrow[t]
-            YT[0, t] = jnp.concatenate([rows_t, zero_rows], axis=0).T.astype(bf16)
-            YT[1, t] = jnp.concatenate([zero_rows, rows_t], axis=0).T.astype(bf16)
+            YT[0, t] = jnp.concatenate([rows_t, zero_rows], axis=0).astype(bf16).T
+            YT[1, t] = jnp.concatenate([zero_rows, rows_t], axis=0).astype(bf16).T
             return carry
 
-        lax.fori_loop(first, first + count, per_tile, 0, unroll=4)
-
-    prepare_sources(0, TILES)
-
-    own_x = [S[c, 0:TILES, :] - 0.5 for c in range(3)]
+        lax.fori_loop(first, first + count, per_tile, 0, unroll=unroll)
+
+    own_x = [mid[c] - 0.5 for c in range(3)]
+    own_line = [line[c] for c in range(3)]
+    own_burgers = [burg[c] for c in range(3)]
+    prepare_sources(0, TILES, own_x, own_line, own_burgers, 8)
+
     field = field_rows(own_x)
     for index, value in enumerate(field):
-        xrow[:, index, :] = value
+        each_tile(xrow, index)[...] = value
     for index in range(len(field), AUG):
-        xrow[:, index, :] = jnp.zeros((TILES, TILE), f32)
+        each_tile(xrow, index)[...] = jnp.zeros((TILES, TILE), f32)
 
     def field_tile(t, carry):
         rows_t = xrow[t]
-        left = jnp.concatenate([rows_t, zero_rows], axis=0)
-        right = jnp.concatenate([zero_rows, rows_t], axis=0)
-        XB[t] = jnp.concatenate([left, right], axis=1).astype(bf16)
+        XL[t] = jnp.concatenate([rows_t, zero_rows], axis=0).astype(bf16)
+        XR[t] = jnp.concatenate([zero_rows, rows_t], axis=0).astype(bf16)
         return carry
 
-    lax.fori_loop(0, TILES, field_tile, 0, unroll=4)
+    lax.fori_loop(0, TILES, field_tile, 0, unroll=8)
     FT[POOL] = jnp.zeros((3 * FEATURES, TILE), bf16)
 
     pl.semaphore_wait(barrier, 8)
     for copy in ghost_copies:
         copy.start()
 
-    scaled = [2.0 * (S[c, 0:TILES, :] - 0.5) for c in range(3)]
+    scaled = [2.0 * (mid[c] - 0.5) for c in range(3)]
     powers = []
     for u in scaled:
         square = u * u
         powers.append([jnp.ones_like(u), u, square, square * u, square * square])
     for r, (e0, e1, e2) in enumerate(exponent_table()):
-        mono[:, r, :] = powers[0][e0] * powers[1][e1] * powers[2][e2]
+        each_tile(mono, r)[...] = powers[0][e0] * powers[1][e1] * powers[2][e2]
     for r in range(35, 40):
-        mono[:, r, :] = jnp.zeros((TILES, TILE), f32)
+        each_tile(mono, r)[...] = jnp.zeros((TILES, TILE), f32)
     for beta in range(3):
         for gamma in range(3):
-            bl[:, 3 * beta + gamma, :] = S[6 + beta, 0:TILES, :] * S[3 + gamma, 0:TILES, :]
+            each_tile(bl, 3 * beta + gamma)[...] = burg[beta] * line[gamma]
     cacc[...] = jnp.zeros_like(cacc)
     sub128 = lax.broadcasted_iota(jnp.int32, (TILE, TILE), 0)
 
@@ -277,7 +301,7 @@
             high = terms.astype(bf16)
             highs.append(high)
             lows.append((terms - high.astype(f32)).astype(bf16))
-            cells = cell_ref[0, :, pl.ds(pl.multiple_of(t * TILE, TILE), TILE)]
+            cells = cells_in[pl.ds(t, 1), :]
             members.append(jnp.where(sub128 == cells, 1.0, 0.0).astype(bf16))
         lhs = jnp.concatenate(
             [jnp.concatenate(highs, axis=1), jnp.concatenate(lows, axis=1)], axis=0
@@ -303,73 +327,84 @@
         ghost_copies[k].wait()
     for q in range(8):
         a, b = neighbour_offsets[q]
-        rows = pl.ds(TILES + GHOST * q, GHOST)
-        S[0, rows, :] = ghost[q, 0] + float(a)
-        S[1, rows, :] = ghost[q, 1] + float(b)
+        rows = pl.ds(GHOST * q, GHOST)
+        far[0, rows, :] = ghost[q, 0] + float(a)
+        far[1, rows, :] = ghost[q, 1] + float(b)
         for c in range(2, 9):
-            S[c, rows, :] = ghost[q, c]
-    prepare_sources(TILES, POOL - TILES)
-
-    def stage_inner(t):
-        rhs = XB[t]
+            far[c, rows, :] = ghost[q, c]
+    prepare_sources(
+        TILES,
+        POOL - TILES,
+        [far[c] - 0.5 for c in range(3)],
+        [far[c] for c in range(3, 6)],
+        [far[c] for c in range(6, 9)],
+        8,
+    )
+
+    def stage_inner(t, slot):
+        rhs = jnp.concatenate([XL[t], XR[t]], axis=1)
         for pair in range(NP // 2):
-            lhs = YT[0, plist[0, 0, t, 2 * pair]] + YT[1, plist[0, 0, t, 2 * pair + 1]]
-            R2[pair] = jnp.dot(lhs, rhs, preferred_element_type=f32)
-
-    def stage_power():
+            lhs = YT[0, plist[2 * pair, 0, t]] + YT[1, plist[2 * pair + 1, 0, t]]
+            R2[slot, pair] = jnp.dot(lhs, rhs, preferred_element_type=f32)
+
+    def stage_power(slot):
         for n in range(NP):
-            radius_sq = R2[n // 2, :, (n % 2) * TILE : (n % 2 + 1) * TILE]
+            radius_sq = R2[slot, n // 2, :, (n % 2) * TILE : (n % 2 + 1) * TILE]
             inverse = lax.rsqrt(radius_sq)
             square = inverse * inverse
             value = square * square * inverse
             high = value.astype(bf16)
-            VS[n * TILE : (n + 1) * TILE, 0:TILE] = high
-            VS[n * TILE : (n + 1) * TILE, TILE : 2 * TILE] = (value - high.astype(f32)).astype(bf16)
-
-    def stage_sum(t):
+            VH[slot, n * TILE : (n + 1) * TILE, :] = high
+            VL[slot, n * TILE : (n + 1) * TILE, :] = (value - high.astype(f32)).astype(bf16)
+
+    def stage_sum(t, slot):
         count = pcount[0, 0, t]
         chosen = []
         for n in range(NP):
             valid = jnp.minimum(jnp.maximum(count - n, 0), 1)
-            chosen.append(FT[valid * (plist[0, 0, t, n] - POOL) + POOL])
-        total = jnp.dot(jnp.concatenate(chosen, axis=1), VS[...], preferred_element_type=f32)
+            chosen.append(FT[valid * (plist[n, 0, t] - POOL) + POOL])
+        weights = jnp.concatenate([VH[slot], VL[slot]], axis=1)
+        total = jnp.dot(jnp.concatenate(chosen, axis=1), weights, preferred_element_type=f32)
         total = total[:, 0:TILE] + total[:, TILE : 2 * TILE]
         MT[t] = total[0:FEATURES] + total[FEATURES : 2 * FEATURES] + total[2 * FEATURES : 3 * FEATURES]
 
-    stage_inner(0)
-    stage_power()
-    stage_inner(1)
-
-    def pair_step(t, carry):
-        stage_sum(t - 2)
-        stage_power()
-        stage_inner(t)
+    stage_inner(0, 0)
+    stage_power(0)
+    stage_inner(1, 1)
+
+    def pair_steps(step, carry):
+        for inner in range(UNROLL):
+            t = step * UNROLL + inner + 2
+            stage_sum(t - 2, inner % 2)
+            stage_power((inner + 1) % 2)
+            stage_inner(t, inner % 2)
         return carry
 
-    lax.fori_loop(2, TILES, pair_step, 0)
-    stage_sum(TILES - 2)
-    stage_power()
-    stage_sum(TILES - 1)
-
-    x = [S[c, 0:TILES, :] - 0.5 for c in range(3)]
-    stress = stress_from_moments(x, [MT[:, r, :] for r in range(36)])
-    burgers = [S[6 + c, 0:TILES, :] for c in range(3)]
-    line = [S[3 + c, 0:TILES, :] for c in range(3)]
-    traction = [dot3([stress[SYM[(m, n)]] for n in range(3)], burgers) for m in range(3)]
-    force = cross(traction, line)
+    lax.fori_loop(0, (TILES - 2) // UNROLL, pair_steps, 0)
+    stage_sum(TILES - 2, 0)
+    stage_power(1)
+    stage_sum(TILES - 1, 1)
+
+    own_x = [mid[c] - 0.5 for c in range(3)]
+    own_line = [line[c] for c in range(3)]
+    own_burgers = [burg[c] for c in range(3)]
+    stress = stress_from_moments(own_x, [each_tile(MT, r)[...] for r in range(36)])
+    traction = [dot3([stress[SYM[(m, n)]] for n in range(3)], own_burgers) for m in range(3)]
+    force = cross(traction, own_line)
     for c in range(3):
         for piece, value in enumerate(pieces(0.5 * force[c], 2)):
-            frow[:, 2 * c + piece, :] = value
+            each_tile(frow, 2 * c + piece)[...] = value
     nacc[...] = jnp.zeros_like(nacc)
     sub40 = lax.broadcasted_iota(jnp.int32, (40, TILE), 0)
 
     def node_group(group, carry):
         lefts, rights = [], []
-        for inner in range(4):
-            t = group * 4 + inner
+        for inner in range(NODE_GROUP):
+            t = group * NODE_GROUP + inner
             rows_t = frow[t]
+            ends = nodes_in[t]
             for end in range(2):
-                nodes = node_ref[0, 0, end : end + 1, pl.ds(pl.multiple_of(t * TILE, TILE), TILE)]
+                nodes = ends[end : end + 1, :]
                 outer = sub40 == lax.shift_right_logical(nodes, 7)
                 lefts.append(
                     jnp.concatenate(
@@ -385,7 +420,7 @@
         )
         return carry
 
-    lax.fori_loop(0, TILES // 4, node_group, 0)
+    lax.fori_loop(0, TILES // NODE_GROUP, node_group, 0)
     for c in range(3):
         total = nacc[80 * c : 80 * c + 40, :] + nacc[80 * c + 40 : 80 * c + 80, :]
         for d in range(9):
@@ -399,47 +434,65 @@
     moments = cpkt[4]
     for q in range(8):
         moments = moments + crecv[q]
-    turned = []
-    for block in range(3):
-        part = moments[:, block * TILE : (block + 1) * TILE]
-        part = jnp.concatenate([part, jnp.zeros((TILE - CELL_DEV, TILE), f32)], axis=0)
-        turned.append(part.T)
-    turned = jnp.concatenate(turned, axis=0)
     for k in range(9):
-        cout_ref[35 * k : 35 * k + 35, :] = turned[40 * k : 40 * k + 35, 0:CELL_DEV]
+        cout_ref[:, 35 * k : 35 * k + 35] = moments[:, 40 * k : 40 * k + 35]
     for copy in node_copies:
         copy.wait()
     nodes = npkt[4]
     for q in range(8):
         nodes = nodes + nrecv[q]
-    for quarter in range(4):
-        nout_ref[0, 0, :, quarter * TILE : (quarter + 1) * TILE] = nodes[:, quarter, :]
-
-
-def on_device(*arguments):
+    nout_ref[...] = nodes
+
+
+def on_device(
+    seg_mid, seg_line, seg_burgers, seg_cell, seg_node, ghost_list, ghost_count, pair_list, pair_count
+):
+    shape3 = (3, TILES, TILE)
+    arguments = (
+        seg_mid.reshape(shape3),
+        seg_line.reshape(shape3),
+        seg_burgers.reshape(shape3),
+        seg_cell.reshape(TILES, TILE),
+        seg_node.reshape(2, TILES, TILE).transpose(1, 0, 2),
+        ghost_list.reshape(8, GHOST).T,
+        ghost_count,
+        pair_list.transpose(3, 0, 1, 2).reshape(NP, 1, TILES),
+        pair_count,
+    )
     vmem = pl.BlockSpec(memory_space=pltpu.VMEM)
-    smem = pl.BlockSpec(memory_space=pltpu.SMEM)
-    return pl.pallas_call(
+    anywhere = pl.BlockSpec(memory_space=pl.ANY)
+    node_force, moments = pl.pallas_call(
         kernel,
         out_shape=(
-            jax.ShapeDtypeStruct((1, 1, 3, NODE_DEV), f32),
-            jax.ShapeDtypeStruct((COMPONENTS, CELL_DEV), f32),
+            jax.ShapeDtypeStruct((3, NODE_DEV // TILE, TILE), f32),
+            jax.ShapeDtypeStruct((CELL_DEV, COMPONENTS), f32),
         ),
-        in_specs=[vmem] * 5 + [smem] * 4,
+        in_specs=[anywhere] * 9,
         out_specs=(vmem, vmem),
         scratch_shapes=[
-            pltpu.VMEM((9, POOL, TILE), f32),
-            pltpu.VMEM((TILES, 9, TILE), f32),
+            pltpu.VMEM(shape3, f32),
+            pltpu.VMEM(shape3, f32),
+            pltpu.VMEM(shape3, f32),
+            pltpu.VMEM((TILES, TILE), jnp.int32),
+            pltpu.VMEM((TILES, 2, TILE), jnp.int32),
+            pltpu.SMEM((GHOST, 8), jnp.int32),
+            pltpu.SMEM((1, 1, 8), jnp.int32),
+            pltpu.SMEM((NP, 1, TILES), jnp.int32),
+            pltpu.SMEM((1, 1, TILES), jnp.int32),
+            pltpu.VMEM((TILES, 16, TILE), f32),
             pltpu.VMEM((8, 9, GHOST, TILE), f32),
             pltpu.VMEM((8, 9, GHOST, TILE), f32),
+            pltpu.VMEM((9, POOL - TILES, TILE), f32),
             pltpu.VMEM((POOL, FEATURES, TILE), f32),
             pltpu.VMEM((POOL + 1, 3 * FEATURES, TILE), bf16),
             pltpu.VMEM((POOL, AUG, TILE), f32),
             pltpu.VMEM((2, POOL, TILE, 2 * AUG), bf16),
             pltpu.VMEM((TILES, AUG, TILE), f32),
-            pltpu.VMEM((TILES, 2 * AUG, 2 * TILE), bf16),
-            pltpu.VMEM((NP // 2, TILE, 2 * TILE), f32),
-            pltpu.VMEM((NP * TILE, 2 * TILE), bf16),
+            pltpu.VMEM((TILES, 2 * AUG, TILE), bf16),
+            pltpu.VMEM((TILES, 2 * AUG, TILE), bf16),
+            pltpu.VMEM((2, NP // 2, TILE, 2 * TILE), f32),
+            pltpu.VMEM((2, NP * TILE, TILE), bf16),
+            pltpu.VMEM((2, NP * TILE, TILE), bf16),
             pltpu.VMEM((TILES, FEATURES, TILE), f32),
             pltpu.VMEM((TILES, 40, TILE), f32),
             pltpu.VMEM((TILES, 16, TILE), f32),
@@ -452,10 +505,14 @@
             pltpu.VMEM((8, 3, 4, TILE), f32),
             pltpu.SemaphoreType.DMA((3, 8)),
             pltpu.SemaphoreType.DMA((3, 8)),
+            pltpu.SemaphoreType.DMA((9,)),
         ],
-        compiler_params=pltpu.CompilerParams(collective_id=0, has_side_effects=True, vmem_limit_bytes=48 * 1024 * 1024),
+        compiler_params=pltpu.CompilerParams(
+            collective_id=0, has_side_effects=True, vmem_limit_bytes=60 * 1024 * 1024
+        ),
         name="segments",
     )(*arguments)
+    return node_force.reshape(1, 1, 3, NODE_DEV), moments.T
 
 
 def solution(mesh):

time: 47.1 us -> 40.2 us (0.85)
  Pallas kernels: 40.9 us -> 37.5 us
  local copies, waits for them, and re-layouts: 5.21 us -> 1.89 us
    pallas_call x1, Pallas kernels: 40.9 us -> 37.5 us  [on_device(): pl.pallas_call(kernel, out_shape=(jax.ShapeDtypeStruct((3, NODE_DEV // TI...]
    unnamed x17 -> x4, local copies, waits for them, and re-layouts: 3.91 us -> 1.89 us
    pallas_call x2 -> x0, local copies, waits for them, and re-layouts: 1.3 us -> none  [on_device(): pl.pallas_call(kernel, out_shape=(jax.ShapeDtypeStruct((1, 1, 3, NODE_DEV...]
where the time goes in v2:
time: 40.2 us; the launch traced here: 40 us
  Pallas kernels  37.5 us (93%)
  local copies, waits for them, and re-layouts  1.89 us (5%)
  between operations  0.65 us (2%)
    pallas_call x1, Pallas kernels, on_device(): pl.pallas_call(kernel, out_shape=(jax.ShapeDtypeStruct((3, NODE_DEV // TI...  37.5 us
    unnamed x4, local copies, waits for them, and re-layouts  1.89 us

profile of v2, /device:TPU:1, one launch (start us, length us, event | category | flops | bytes accessed | tf_op | source)
XLA Modules:
  0.0 40.0 jit_solution(977277868587920601)
XLA Ops:
  0.6 37.5 %segments.1 = (f32[3,4,128]{2,1,0:T(4,128)}, f32[8,315]{1,0:T(8,128)}) custom-call(f32[3,32,128]{2,1,0:T(8,128)} %bitcast.17, f32[3,32,128]{2,1,0:T(8,128)} %bitcast.18, f32[3,32,128]{2,1,0:T(8,128)} %bitcast.19, s32[32,128]{1,0:T(8,128)} %bitcast.21, s32[32,2,128]{2,1,0:T(2,128)} %bitcast.20, s32[2,8]{1,0:T(2,128)} %bitcast.25, s32[1,1,8]{2,1,0:T(1,128)} %gcount_any.1, ...), custom_call_target="tpu_custom_call" | custom-call | tf_op jit(solution)/shard_map/segments/pallas_call | solution.py:464
  38.1 0.0 copy-start
  38.1 1.3 %copy.17 = f32[1,1,3,512]{3,1,2,0:T(1,128)} copy(f32[1,1,3,512]{3,1,2,0:T(1,128)} %bitcast.24) | data formatting | bytes 12288
  39.4 0.0 copy-done
  39.4 0.6 %copy.18 = f32[315,8]{0,1:T(8,128)} copy(f32[315,8]{0,1:T(8,128)S(1)} %bitcast.22) | data formatting | bytes 20160
Async XLA Ops:
  38.1 1.3 %copy-start = (f32[8,315]{1,0:T(8,128)S(1)}, f32[8,315]{1,0:T(8,128)}, u32[]{:S(2)}) copy-start(f32[8,315]{1,0:T(8,128)} %get-tuple-element.5) | copy-start | bytes 30244

commit v3 on v2

--- a/solution.py
+++ b/solution.py
@@ -15,7 +15,7 @@
 POOL = 48
 FEATURES = 40
 AUG = 32
-UNROLL = 6
+UNROLL = 10
 NODE_GROUP = 16
 TERMS = 368
 
@@ -42,9 +42,12 @@
     return parts
 
 
-def each_tile(ref, index, first=0, count=TILES):
-    blocks, pitch, lanes = ref.shape
-    return ref.reshape(blocks * pitch, lanes).at[pl.ds(first * pitch + index, count, stride=pitch), :]
+def each_tile(ref, pitch, index, first=0, count=TILES):
+    return ref.at[pl.ds(first * pitch + index, count, stride=pitch), :]
+
+
+def tile_rows(ref, pitch, t, rows):
+    return ref.at[pl.ds(t * pitch, rows), :]
 
 
 def exponent_table():
@@ -218,10 +221,11 @@
     for load in loads:
         load.wait()
 
+    own_flat = own.reshape(TILES * 16, TILE)
     for c in range(3):
-        each_tile(own, c)[...] = mid[c]
-        each_tile(own, 3 + c)[...] = line[c]
-        each_tile(own, 6 + c)[...] = burg[c]
+        each_tile(own_flat, 16, c)[...] = mid[c]
+        each_tile(own_flat, 16, 3 + c)[...] = line[c]
+        each_tile(own_flat, 16, 6 + c)[...] = burg[c]
     for k in range(8):
         for g in range(GHOST):
             valid = jnp.minimum(jnp.maximum(gcount[0, 0, k] - g, 0), 1).astype(f32)
@@ -232,18 +236,18 @@
 
     def prepare_sources(first, count, y, line_rows, burgers, unroll):
         for index, value in enumerate(source_features(y, line_rows, burgers)):
-            each_tile(feat, index, first, count)[...] = value
+            each_tile(feat, 41, index, first, count)[...] = value
         for index, value in enumerate(source_rows(y)):
-            each_tile(yrow, index, first, count)[...] = value
+            each_tile(yrow, 33, index, first, count)[...] = value
         zero = jnp.zeros_like(y[0])
         for index in range(36, FEATURES):
-            each_tile(feat, index, first, count)[...] = zero
+            each_tile(feat, 41, index, first, count)[...] = zero
         for index in range(24, AUG):
-            each_tile(yrow, index, first, count)[...] = zero
+            each_tile(yrow, 33, index, first, count)[...] = zero
 
         def per_tile(t, carry):
-            FT[t] = jnp.concatenate(pieces(feat[t], 3), axis=0).astype(bf16)
-            rows_t = yrow[t]
+            FT[t] = jnp.concatenate(pieces(tile_rows(feat, 41, t, FEATURES)[...], 3), axis=0).astype(bf16)
+            rows_t = tile_rows(yrow, 33, t, AUG)[...]
             YT[0, t] = jnp.concatenate([rows_t, zero_rows], axis=0).astype(bf16).T
             YT[1, t] = jnp.concatenate([zero_rows, rows_t], axis=0).astype(bf16).T
             return carry
@@ -257,12 +261,12 @@
 
     field = field_rows(own_x)
     for index, value in enumerate(field):
-        each_tile(xrow, index)[...] = value
+        each_tile(xrow, 33, index)[...] = value
     for index in range(len(field), AUG):
-        each_tile(xrow, index)[...] = jnp.zeros((TILES, TILE), f32)
+        each_tile(xrow, 33, index)[...] = jnp.zeros((TILES, TILE), f32)
 
     def field_tile(t, carry):
-        rows_t = xrow[t]
+        rows_t = tile_rows(xrow, 33, t, AUG)[...]
         XL[t] = jnp.concatenate([rows_t, zero_rows], axis=0).astype(bf16)
         XR[t] = jnp.concatenate([zero_rows, rows_t], axis=0).astype(bf16)
         return carry
@@ -280,12 +284,12 @@
         square = u * u
         powers.append([jnp.ones_like(u), u, square, square * u, square * square])
     for r, (e0, e1, e2) in enumerate(exponent_table()):
-        each_tile(mono, r)[...] = powers[0][e0] * powers[1][e1] * powers[2][e2]
+        each_tile(mono, 41, r)[...] = powers[0][e0] * powers[1][e1] * powers[2][e2]
     for r in range(35, 40):
-        each_tile(mono, r)[...] = jnp.zeros((TILES, TILE), f32)
+        each_tile(mono, 41, r)[...] = jnp.zeros((TILES, TILE), f32)
     for beta in range(3):
         for gamma in range(3):
-            each_tile(bl, 3 * beta + gamma)[...] = burg[beta] * line[gamma]
+            each_tile(bl, 9, 3 * beta + gamma)[...] = burg[beta] * line[gamma]
     cacc[...] = jnp.zeros_like(cacc)
     sub128 = lax.broadcasted_iota(jnp.int32, (TILE, TILE), 0)
 
@@ -293,8 +297,8 @@
         highs, lows, members = [], [], []
         for inner in range(4):
             t = group * 4 + inner
-            mono_t = mono[t]
-            bl_t = bl[t]
+            mono_t = tile_rows(mono, 41, t, 40)[...]
+            bl_t = tile_rows(bl, 9, t, 9)[...]
             block = [bl_t[k : k + 1, :] * mono_t for k in range(9)]
             block.append(jnp.zeros((8, TILE), f32))
             terms = jnp.concatenate(block, axis=0)
@@ -366,7 +370,7 @@
         weights = jnp.concatenate([VH[slot], VL[slot]], axis=1)
         total = jnp.dot(jnp.concatenate(chosen, axis=1), weights, preferred_element_type=f32)
         total = total[:, 0:TILE] + total[:, TILE : 2 * TILE]
-        MT[t] = total[0:FEATURES] + total[FEATURES : 2 * FEATURES] + total[2 * FEATURES : 3 * FEATURES]
+        tile_rows(MT, 41, t, FEATURES)[...] = total[0:FEATURES] + total[FEATURES : 2 * FEATURES] + total[2 * FEATURES : 3 * FEATURES]
 
     stage_inner(0, 0)
     stage_power(0)
@@ -388,12 +392,12 @@
     own_x = [mid[c] - 0.5 for c in range(3)]
     own_line = [line[c] for c in range(3)]
     own_burgers = [burg[c] for c in range(3)]
-    stress = stress_from_moments(own_x, [each_tile(MT, r)[...] for r in range(36)])
+    stress = stress_from_moments(own_x, [each_tile(MT, 41, r)[...] for r in range(36)])
     traction = [dot3([stress[SYM[(m, n)]] for n in range(3)], own_burgers) for m in range(3)]
     force = cross(traction, own_line)
     for c in range(3):
         for piece, value in enumerate(pieces(0.5 * force[c], 2)):
-            each_tile(frow, 2 * c + piece)[...] = value
+            each_tile(frow, 9, 2 * c + piece)[...] = value
     nacc[...] = jnp.zeros_like(nacc)
     sub40 = lax.broadcasted_iota(jnp.int32, (40, TILE), 0)
 
@@ -401,7 +405,7 @@
         lefts, rights = [], []
         for inner in range(NODE_GROUP):
             t = group * NODE_GROUP + inner
-            rows_t = frow[t]
+            rows_t = tile_rows(frow, 9, t, 6)[...]
             ends = nodes_in[t]
             for end in range(2):
                 nodes = ends[end : end + 1, :]
@@ -483,23 +487,23 @@
             pltpu.VMEM((8, 9, GHOST, TILE), f32),
             pltpu.VMEM((8, 9, GHOST, TILE), f32),
             pltpu.VMEM((9, POOL - TILES, TILE), f32),
-            pltpu.VMEM((POOL, FEATURES, TILE), f32),
+            pltpu.VMEM((POOL * 41, TILE), f32),
             pltpu.VMEM((POOL + 1, 3 * FEATURES, TILE), bf16),
-            pltpu.VMEM((POOL, AUG, TILE), f32),
+            pltpu.VMEM((POOL * 33, TILE), f32),
             pltpu.VMEM((2, POOL, TILE, 2 * AUG), bf16),
-            pltpu.VMEM((TILES, AUG, TILE), f32),
+            pltpu.VMEM((TILES * 33, TILE), f32),
             pltpu.VMEM((TILES, 2 * AUG, TILE), bf16),
             pltpu.VMEM((TILES, 2 * AUG, TILE), bf16),
             pltpu.VMEM((2, NP // 2, TILE, 2 * TILE), f32),
             pltpu.VMEM((2, NP * TILE, TILE), bf16),
             pltpu.VMEM((2, NP * TILE, TILE), bf16),
-            pltpu.VMEM((TILES, FEATURES, TILE), f32),
-            pltpu.VMEM((TILES, 40, TILE), f32),
-            pltpu.VMEM((TILES, 16, TILE), f32),
+            pltpu.VMEM((TILES * 41, TILE), f32),
+            pltpu.VMEM((TILES * 41, TILE), f32),
+            pltpu.VMEM((TILES * 9, TILE), f32),
             pltpu.VMEM((2 * TERMS, TILE), f32),
             pltpu.VMEM((9, CELL_DEV, 384), f32),
             pltpu.VMEM((8, CELL_DEV, 384), f32),
-            pltpu.VMEM((TILES, 8, TILE), f32),
+            pltpu.VMEM((TILES * 9, TILE), f32),
             pltpu.VMEM((240, TILE), f32),
             pltpu.VMEM((9, 3, 4, TILE), f32),
             pltpu.VMEM((8, 3, 4, TILE), f32),
@@ -508,10 +512,10 @@
             pltpu.SemaphoreType.DMA((9,)),
         ],
         compiler_params=pltpu.CompilerParams(
-            collective_id=0, has_side_effects=True, vmem_limit_bytes=60 * 1024 * 1024
+            collective_id=0, has_side_effects=True, vmem_limit_bytes=40 * 1024 * 1024
         ),
         name="segments",
-    )(*arguments)
+    )(*[pltpu.with_memory_space_constraint(value, pltpu.HBM) for value in arguments])
     return node_force.reshape(1, 1, 3, NODE_DEV), moments.T
 
 

time: 40.2 us -> 37.3 us (0.928)
  Pallas kernels: 37.5 us -> 35.3 us
  local copies, waits for them, and re-layouts: 1.89 us -> 1.19 us
    pallas_call x1, Pallas kernels: 37.5 us -> 35.3 us  [on_device(): pl.pallas_call(kernel, out_shape=(jax.ShapeDtypeStruct((3, NODE_DEV // TI...]
    unnamed x4 -> x2, local copies, waits for them, and re-layouts: 1.89 us -> 1.19 us
where the time goes in v3:
time: 37.3 us; the launch traced here: 37.1 us
  Pallas kernels  35.3 us (95%)
  local copies, waits for them, and re-layouts  1.19 us (3%)
  between operations  0.64 us (2%)
    pallas_call x1, Pallas kernels, on_device(): pl.pallas_call(kernel, out_shape=(jax.ShapeDtypeStruct((3, NODE_DEV // TI...  35.3 us
    unnamed x2, local copies, waits for them, and re-layouts  1.19 us

profile of v3, /device:TPU:1, one launch (start us, length us, event | category | flops | bytes accessed | tf_op | source)
XLA Modules:
  0.0 37.1 jit_solution(7936210938738159551)
XLA Ops:
  0.6 35.3 %segments.1 = (f32[3,4,128]{2,1,0:T(4,128)S(1)}, f32[8,315]{1,0:T(8,128)S(1)}) custom-call(f32[3,32,128]{2,1,0:T(8,128)} %bitcast.19, f32[3,32,128]{2,1,0:T(8,128)} %bitcast.20, f32[3,32,128]{2,1,0:T(8,128)} %bitcast.21, s32[32,128]{1,0:T(8,128)} %bitcast.23, s32[32,2,128]{2,1,0:T(2,128)} %bitcast.22, s32[2,8]{1,0:T(2,128)} %bitcast.25, ...), custom_call_target="tpu_custom_call" | custom-call | tf_op jit(solution)/shard_map/segments/pallas_call | solution.py:468
  35.9 0.6 %copy.17 = f32[1,1,3,512]{3,1,2,0:T(1,128)} copy(f32[1,1,3,512]{3,1,2,0:T(1,128)S(1)} %bitcast.18) | data formatting | bytes 12288
  36.5 0.6 %copy.18 = f32[315,8]{0,1:T(8,128)} copy(f32[315,8]{0,1:T(8,128)S(1)} %bitcast.17) | data formatting | bytes 20160

commit v4 on v3

--- a/solution.py
+++ b/solution.py
@@ -15,8 +15,9 @@
 POOL = 48
 FEATURES = 40
 AUG = 32
-UNROLL = 10
+UNROLL = 30
 NODE_GROUP = 16
+NODE_ROWS = 216
 TERMS = 368
 
 core_radius = 0.1
@@ -25,6 +26,7 @@
 f32 = jnp.float32
 bf16 = jnp.bfloat16
 MESH = pl.DeviceIdType.MESH
+SEND_ORDER = (0, 2, 5, 7, 1, 6, 3, 4)
 NT = (((1,), (1,)), ((), ()))
 
 
@@ -275,8 +277,8 @@
     FT[POOL] = jnp.zeros((3 * FEATURES, TILE), bf16)
 
     pl.semaphore_wait(barrier, 8)
-    for copy in ghost_copies:
-        copy.start()
+    for k in SEND_ORDER:
+        ghost_copies[k].start()
 
     scaled = [2.0 * (mid[c] - 0.5) for c in range(3)]
     powers = []
@@ -324,8 +326,8 @@
         for d in range(9):
             cpkt[d, :, block * TILE : (block + 1) * TILE] = turned[8 * d : 8 * d + 8, :]
     cell_copies = sends(1, lambda k: cpkt.at[k + (k >= 4)], crecv)
-    for copy in cell_copies:
-        copy.start()
+    for k in SEND_ORDER:
+        cell_copies[k].start()
 
     for k in range(8):
         ghost_copies[k].wait()
@@ -342,7 +344,7 @@
         [far[c] - 0.5 for c in range(3)],
         [far[c] for c in range(3, 6)],
         [far[c] for c in range(6, 9)],
-        8,
+        16,
     )
 
     def stage_inner(t, slot):
@@ -397,24 +399,22 @@
     force = cross(traction, own_line)
     for c in range(3):
         for piece, value in enumerate(pieces(0.5 * force[c], 2)):
-            each_tile(frow, 9, 2 * c + piece)[...] = value
+            for copy_index in range(4):
+                each_tile(frow, 25, 6 * copy_index + 2 * c + piece)[...] = value
     nacc[...] = jnp.zeros_like(nacc)
-    sub40 = lax.broadcasted_iota(jnp.int32, (40, TILE), 0)
+    row_node = lax.broadcasted_iota(jnp.int32, (NODE_ROWS, TILE), 0) // 6
 
     def node_group(group, carry):
         lefts, rights = [], []
         for inner in range(NODE_GROUP):
             t = group * NODE_GROUP + inner
-            rows_t = tile_rows(frow, 9, t, 6)[...]
+            rows_t = tile_rows(frow, 25, t, 24)[...]
+            rows_t = jnp.concatenate([rows_t] * 9, axis=0)
             ends = nodes_in[t]
             for end in range(2):
                 nodes = ends[end : end + 1, :]
-                outer = sub40 == lax.shift_right_logical(nodes, 7)
-                lefts.append(
-                    jnp.concatenate(
-                        [jnp.where(outer, rows_t[r : r + 1, :], 0.0) for r in range(6)], axis=0
-                    ).astype(bf16)
-                )
+                outer = row_node == lax.shift_right_logical(nodes, 7)
+                lefts.append(jnp.where(outer, rows_t, 0.0).astype(bf16))
                 rights.append(jnp.where(sub128 == (nodes & 127), 1.0, 0.0).astype(bf16))
         nacc[...] += lax.dot_general(
             jnp.concatenate(lefts, axis=1),
@@ -425,13 +425,13 @@
         return carry
 
     lax.fori_loop(0, TILES // NODE_GROUP, node_group, 0)
-    for c in range(3):
-        total = nacc[80 * c : 80 * c + 40, :] + nacc[80 * c + 40 : 80 * c + 80, :]
-        for d in range(9):
-            npkt[d, c] = total[4 * d : 4 * d + 4, :]
+    for d in range(9):
+        for c in range(3):
+            first = 24 * d + 2 * c
+            npkt[d, c] = nacc[pl.ds(first, 4, stride=6), :] + nacc[pl.ds(first + 1, 4, stride=6), :]
     node_copies = sends(2, lambda k: npkt.at[k + (k >= 4)], nrecv)
-    for copy in node_copies:
-        copy.start()
+    for k in SEND_ORDER:
+        node_copies[k].start()
 
     for copy in cell_copies:
         copy.wait()
@@ -446,6 +446,11 @@
     for q in range(8):
         nodes = nodes + nrecv[q]
     nout_ref[...] = nodes
+
+
+def hand_over(node_in, moments_in, node_out, moments_out):
+    node_out[...] = node_in[...]
+    moments_out[...] = moments_in[...]
 
 
 def on_device(
@@ -503,8 +508,8 @@
             pltpu.VMEM((2 * TERMS, TILE), f32),
             pltpu.VMEM((9, CELL_DEV, 384), f32),
             pltpu.VMEM((8, CELL_DEV, 384), f32),
-            pltpu.VMEM((TILES * 9, TILE), f32),
-            pltpu.VMEM((240, TILE), f32),
+            pltpu.VMEM((TILES * 25, TILE), f32),
+            pltpu.VMEM((NODE_ROWS, TILE), f32),
             pltpu.VMEM((9, 3, 4, TILE), f32),
             pltpu.VMEM((8, 3, 4, TILE), f32),
             pltpu.SemaphoreType.DMA((3, 8)),
@@ -516,6 +521,17 @@
         ),
         name="segments",
     )(*[pltpu.with_memory_space_constraint(value, pltpu.HBM) for value in arguments])
+    node_force, moments = pl.pallas_call(
+        hand_over,
+        out_shape=(
+            jax.ShapeDtypeStruct(node_force.shape, f32),
+            jax.ShapeDtypeStruct(moments.shape, f32),
+        ),
+        in_specs=[vmem, vmem],
+        out_specs=(vmem, vmem),
+        compiler_params=pltpu.CompilerParams(vmem_limit_bytes=1024 * 1024),
+        name="outputs",
+    )(node_force, moments)
     return node_force.reshape(1, 1, 3, NODE_DEV), moments.T
 
 

time: 37.3 us -> 35 us (0.938)
  local copies, waits for them, and re-layouts: 1.19 us -> 0 us
  Pallas kernels: 35.3 us -> 34.2 us
    pallas_call x1, Pallas kernels: 35.3 us -> 33.6 us  [on_device(): pl.pallas_call(kernel, out_shape=(jax.ShapeDtypeStruct((3, NODE_DEV // TI...]
    unnamed x2 -> x0, local copies, waits for them, and re-layouts: 1.19 us -> none
    pallas_call x0 -> x1, Pallas kernels: none -> 0.61 us  [on_device(): pl.pallas_call(hand_over, out_shape=(jax.ShapeDtypeStruct(node_force.shap...]
where the time goes in v4:
time: 35 us; the launch traced here: 34.9 us
  Pallas kernels  34.2 us (98%)
  between operations  0.64 us (2%)
    pallas_call x1, Pallas kernels, on_device(): pl.pallas_call(kernel, out_shape=(jax.ShapeDtypeStruct((3, NODE_DEV // TI...  33.6 us

profile of v4, /device:TPU:1, one launch (start us, length us, event | category | flops | bytes accessed | tf_op | source)
XLA Modules:
  0.0 34.9 jit_solution(13290223695406787313)
XLA Ops:
  0.6 33.6 %segments.1 = (f32[3,4,128]{2,1,0:T(4,128)S(1)}, f32[8,315]{1,0:T(8,128)S(1)}) custom-call(f32[3,32,128]{2,1,0:T(8,128)} %bitcast.17, f32[3,32,128]{2,1,0:T(8,128)} %bitcast.18, f32[3,32,128]{2,1,0:T(8,128)} %bitcast.19, s32[32,128]{1,0:T(8,128)} %bitcast.21, s32[32,2,128]{2,1,0:T(2,128)} %bitcast.20, s32[2,8]{1,0:T(2,128)} %bitcast.23, ...), custom_call_target="tpu_custom_call" | custom-call | tf_op jit(solution)/shard_map/segments/pallas_call | solution.py:473
  34.2 0.6 %outputs.1 = (f32[3,4,128]{2,1,0:T(4,128)}, f32[8,315]{1,0:T(8,128)}) custom-call(f32[3,4,128]{2,1,0:T(4,128)S(1)} %get-tuple-element.6.node_in, f32[8,315]{1,0:T(8,128)S(1)} %get-tuple-element.7.moments_in), custom_call_target="tpu_custom_call" | custom-call | tf_op jit(solution)/shard_map/outputs/pallas_call | solution.py:524

commit v5 on v4

--- a/solution.py
+++ b/solution.py
@@ -14,9 +14,10 @@
 COMPONENTS = 315
 POOL = 48
 FEATURES = 40
+SUM_ROWS = 112
 AUG = 32
 UNROLL = 30
-NODE_GROUP = 16
+NODE_GROUP = 32
 NODE_ROWS = 216
 TERMS = 368
 
@@ -172,7 +173,7 @@
     mid_any, line_any, burg_any, cell_any, node_any, glist_any, gcount_any, plist_any, pcount_any,
     nout_ref, cout_ref,
     mid, line, burg, cells_in, nodes_in, glist, gcount, plist, pcount,
-    own, pkt, ghost, far, feat, FT, yrow, YT, xrow, XL, XR, R2, VH, VL, MT, mono, bl, cacc, cpkt,
+    own, pkt, ghost, far, feat, FT, yrow, YT, xrow, XL, XR, VH, VL, MT, mono, bl, cacc, cpkt,
     crecv, frow, nacc, npkt, nrecv, send_sem, recv_sem, load_sem,
 ):
     i = lax.axis_index("dx")
@@ -248,10 +249,11 @@
             each_tile(yrow, 33, index, first, count)[...] = zero
 
         def per_tile(t, carry):
-            FT[t] = jnp.concatenate(pieces(tile_rows(feat, 41, t, FEATURES)[...], 3), axis=0).astype(bf16)
+            parts = pieces(tile_rows(feat, 41, t, FEATURES)[...], 3)
+            parts = [part[0:32] for part in parts] + [part[32:36] for part in parts]
+            FT[t] = jnp.concatenate(parts + [zero_rows[0:4]], axis=0).astype(bf16)
             rows_t = tile_rows(yrow, 33, t, AUG)[...]
-            YT[0, t] = jnp.concatenate([rows_t, zero_rows], axis=0).astype(bf16).T
-            YT[1, t] = jnp.concatenate([zero_rows, rows_t], axis=0).astype(bf16).T
+            YT[t] = jnp.concatenate([rows_t, rows_t, zero_rows, zero_rows], axis=0).astype(bf16).T
             return carry
 
         lax.fori_loop(first, first + count, per_tile, 0, unroll=unroll)
@@ -274,7 +276,7 @@
         return carry
 
     lax.fori_loop(0, TILES, field_tile, 0, unroll=8)
-    FT[POOL] = jnp.zeros((3 * FEATURES, TILE), bf16)
+    FT[POOL] = jnp.zeros((SUM_ROWS, TILE), bf16)
 
     pl.semaphore_wait(barrier, 8)
     for k in SEND_ORDER:
@@ -347,21 +349,21 @@
         16,
     )
 
-    def stage_inner(t, slot):
+    first_half = lax.broadcasted_iota(jnp.int32, (TILE, TILE), 1) < AUG
+
+    def stage_power(t, slot):
         rhs = jnp.concatenate([XL[t], XR[t]], axis=1)
         for pair in range(NP // 2):
-            lhs = YT[0, plist[2 * pair, 0, t]] + YT[1, plist[2 * pair + 1, 0, t]]
-            R2[slot, pair] = jnp.dot(lhs, rhs, preferred_element_type=f32)
-
-    def stage_power(slot):
-        for n in range(NP):
-            radius_sq = R2[slot, n // 2, :, (n % 2) * TILE : (n % 2 + 1) * TILE]
-            inverse = lax.rsqrt(radius_sq)
-            square = inverse * inverse
-            value = square * square * inverse
-            high = value.astype(bf16)
-            VH[slot, n * TILE : (n + 1) * TILE, :] = high
-            VL[slot, n * TILE : (n + 1) * TILE, :] = (value - high.astype(f32)).astype(bf16)
+            lhs = jnp.where(first_half, YT[plist[2 * pair, 0, t]], YT[plist[2 * pair + 1, 0, t]])
+            both = jnp.dot(lhs[:, 0 : 2 * AUG], rhs, preferred_element_type=f32)
+            for side in range(2):
+                inverse = lax.rsqrt(both[:, side * TILE : (side + 1) * TILE])
+                square = inverse * inverse
+                value = square * square * inverse
+                high = value.astype(bf16)
+                first = (2 * pair + side) * TILE
+                VH[slot, first : first + TILE, :] = high
+                VL[slot, first : first + TILE, :] = (value - high.astype(f32)).astype(bf16)
 
     def stage_sum(t, slot):
         count = pcount[0, 0, t]
@@ -372,29 +374,32 @@
         weights = jnp.concatenate([VH[slot], VL[slot]], axis=1)
         total = jnp.dot(jnp.concatenate(chosen, axis=1), weights, preferred_element_type=f32)
         total = total[:, 0:TILE] + total[:, TILE : 2 * TILE]
-        tile_rows(MT, 41, t, FEATURES)[...] = total[0:FEATURES] + total[FEATURES : 2 * FEATURES] + total[2 * FEATURES : 3 * FEATURES]
-
-    stage_inner(0, 0)
-    stage_power(0)
-    stage_inner(1, 1)
+        target = tile_rows(MT, 49, t, 48)
+        target[0:32, :] = total[0:32] + total[32:64] + total[64:96]
+        target[32:48, :] = total[96:112]
+
+    stage_power(0, 0)
 
     def pair_steps(step, carry):
         for inner in range(UNROLL):
-            t = step * UNROLL + inner + 2
-            stage_sum(t - 2, inner % 2)
-            stage_power((inner + 1) % 2)
-            stage_inner(t, inner % 2)
+            t = step * UNROLL + inner + 1
+            stage_power(t, (inner + 1) % 2)
+            stage_sum(t - 1, inner % 2)
         return carry
 
     lax.fori_loop(0, (TILES - 2) // UNROLL, pair_steps, 0)
+    stage_power(TILES - 1, 1)
     stage_sum(TILES - 2, 0)
-    stage_power(1)
     stage_sum(TILES - 1, 1)
 
     own_x = [mid[c] - 0.5 for c in range(3)]
     own_line = [line[c] for c in range(3)]
     own_burgers = [burg[c] for c in range(3)]
-    stress = stress_from_moments(own_x, [each_tile(MT, 41, r)[...] for r in range(36)])
+    moments = [each_tile(MT, 49, r)[...] for r in range(32)]
+    for r in range(32, 36):
+        parts = [each_tile(MT, 49, r + 4 * piece)[...] for piece in range(3)]
+        moments.append(parts[0] + parts[1] + parts[2])
+    stress = stress_from_moments(own_x, moments)
     traction = [dot3([stress[SYM[(m, n)]] for n in range(3)], own_burgers) for m in range(3)]
     force = cross(traction, own_line)
     for c in range(3):
@@ -493,16 +498,15 @@
             pltpu.VMEM((8, 9, GHOST, TILE), f32),
             pltpu.VMEM((9, POOL - TILES, TILE), f32),
             pltpu.VMEM((POOL * 41, TILE), f32),
-            pltpu.VMEM((POOL + 1, 3 * FEATURES, TILE), bf16),
+            pltpu.VMEM((POOL + 1, SUM_ROWS, TILE), bf16),
             pltpu.VMEM((POOL * 33, TILE), f32),
-            pltpu.VMEM((2, POOL, TILE, 2 * AUG), bf16),
+            pltpu.VMEM((POOL, TILE, TILE), bf16),
             pltpu.VMEM((TILES * 33, TILE), f32),
             pltpu.VMEM((TILES, 2 * AUG, TILE), bf16),
             pltpu.VMEM((TILES, 2 * AUG, TILE), bf16),
-            pltpu.VMEM((2, NP // 2, TILE, 2 * TILE), f32),
             pltpu.VMEM((2, NP * TILE, TILE), bf16),
             pltpu.VMEM((2, NP * TILE, TILE), bf16),
-            pltpu.VMEM((TILES * 41, TILE), f32),
+            pltpu.VMEM((TILES * 49, TILE), f32),
             pltpu.VMEM((TILES * 41, TILE), f32),
             pltpu.VMEM((TILES * 9, TILE), f32),
             pltpu.VMEM((2 * TERMS, TILE), f32),

time: 35 us -> 34.4 us (0.983)
  Pallas kernels: 34.2 us -> 33.6 us
    pallas_call x1, Pallas kernels: 33.6 us -> 33 us  [on_device(): pl.pallas_call(kernel, out_shape=(jax.ShapeDtypeStruct((3, NODE_DEV // TI...]
where the time goes in v5:
time: 34.4 us; the launch traced here: 34.3 us
  Pallas kernels  33.6 us (98%)
  between operations  0.64 us (2%)
    pallas_call x1, Pallas kernels, on_device(): pl.pallas_call(kernel, out_shape=(jax.ShapeDtypeStruct((3, NODE_DEV // TI...  33 us

profile of v5, /device:TPU:1, one launch (start us, length us, event | category | flops | bytes accessed | tf_op | source)
XLA Modules:
  0.0 34.3 jit_solution(13645087999476288833)
XLA Ops:
  0.6 33.0 %segments.1 = (f32[3,4,128]{2,1,0:T(4,128)S(1)}, f32[8,315]{1,0:T(8,128)S(1)}) custom-call(f32[3,32,128]{2,1,0:T(8,128)} %bitcast.17, f32[3,32,128]{2,1,0:T(8,128)} %bitcast.18, f32[3,32,128]{2,1,0:T(8,128)} %bitcast.19, s32[32,128]{1,0:T(8,128)} %bitcast.21, s32[32,2,128]{2,1,0:T(2,128)} %bitcast.20, s32[2,8]{1,0:T(2,128)} %bitcast.23, ...), custom_call_target="tpu_custom_call" | custom-call | tf_op jit(solution)/shard_map/segments/pallas_call | solution.py:478
  33.7 0.6 %outputs.1 = (f32[3,4,128]{2,1,0:T(4,128)}, f32[8,315]{1,0:T(8,128)}) custom-call(f32[3,4,128]{2,1,0:T(4,128)S(1)} %get-tuple-element.6.node_in, f32[8,315]{1,0:T(8,128)S(1)} %get-tuple-element.7.moments_in), custom_call_target="tpu_custom_call" | custom-call | tf_op jit(solution)/shard_map/outputs/pallas_call | solution.py:528

commit v6 on v5

--- a/solution.py
+++ b/solution.py
@@ -17,7 +17,6 @@
 SUM_ROWS = 112
 AUG = 32
 UNROLL = 30
-NODE_GROUP = 32
 NODE_ROWS = 216
 TERMS = 368
 
@@ -388,31 +387,25 @@
         return carry
 
     lax.fori_loop(0, (TILES - 2) // UNROLL, pair_steps, 0)
-    stage_power(TILES - 1, 1)
-    stage_sum(TILES - 2, 0)
-    stage_sum(TILES - 1, 1)
-
-    own_x = [mid[c] - 0.5 for c in range(3)]
-    own_line = [line[c] for c in range(3)]
-    own_burgers = [burg[c] for c in range(3)]
-    moments = [each_tile(MT, 49, r)[...] for r in range(32)]
-    for r in range(32, 36):
-        parts = [each_tile(MT, 49, r + 4 * piece)[...] for piece in range(3)]
-        moments.append(parts[0] + parts[1] + parts[2])
-    stress = stress_from_moments(own_x, moments)
-    traction = [dot3([stress[SYM[(m, n)]] for n in range(3)], own_burgers) for m in range(3)]
-    force = cross(traction, own_line)
-    for c in range(3):
-        for piece, value in enumerate(pieces(0.5 * force[c], 2)):
-            for copy_index in range(4):
-                each_tile(frow, 25, 6 * copy_index + 2 * c + piece)[...] = value
-    nacc[...] = jnp.zeros_like(nacc)
     row_node = lax.broadcasted_iota(jnp.int32, (NODE_ROWS, TILE), 0) // 6
 
-    def node_group(group, carry):
+    def scatter(first, count):
+        rows = slice(first, first + count)
+        x = [mid[c, rows] - 0.5 for c in range(3)]
+        moments = [each_tile(MT, 49, r, first, count)[...] for r in range(32)]
+        for r in range(32, 36):
+            parts = [each_tile(MT, 49, r + 4 * piece, first, count)[...] for piece in range(3)]
+            moments.append(parts[0] + parts[1] + parts[2])
+        stress = stress_from_moments(x, moments)
+        burgers = [burg[c, rows] for c in range(3)]
+        traction = [dot3([stress[SYM[(m, n)]] for n in range(3)], burgers) for m in range(3)]
+        force = cross(traction, [line[c, rows] for c in range(3)])
+        for c in range(3):
+            for piece, value in enumerate(pieces(0.5 * force[c], 2)):
+                for copy_index in range(4):
+                    each_tile(frow, 25, 6 * copy_index + 2 * c + piece, first, count)[...] = value
         lefts, rights = [], []
-        for inner in range(NODE_GROUP):
-            t = group * NODE_GROUP + inner
+        for t in range(first, first + count):
             rows_t = tile_rows(frow, 25, t, 24)[...]
             rows_t = jnp.concatenate([rows_t] * 9, axis=0)
             ends = nodes_in[t]
@@ -421,15 +414,19 @@
                 outer = row_node == lax.shift_right_logical(nodes, 7)
                 lefts.append(jnp.where(outer, rows_t, 0.0).astype(bf16))
                 rights.append(jnp.where(sub128 == (nodes & 127), 1.0, 0.0).astype(bf16))
-        nacc[...] += lax.dot_general(
+        return lax.dot_general(
             jnp.concatenate(lefts, axis=1),
             jnp.concatenate(rights, axis=1),
             NT,
             preferred_element_type=f32,
         )
-        return carry
-
-    lax.fori_loop(0, TILES // NODE_GROUP, node_group, 0)
+
+    stage_power(TILES - 1, 1)
+    early = scatter(0, TILES // 2)
+    stage_sum(TILES - 2, 0)
+    stage_sum(TILES - 1, 1)
+
+    nacc[...] = early + scatter(TILES // 2, TILES // 2)
     for d in range(9):
         for c in range(3):
             first = 24 * d + 2 * c

time: 34.4 us -> 34.6 us (level)
  no operation moved by 1% of the time
where the time goes in v6:
time: 34.6 us; the launch traced here: 34.4 us
  Pallas kernels  33.8 us (98%)
  between operations  0.64 us (2%)
    pallas_call x1, Pallas kernels, on_device(): pl.pallas_call(kernel, out_shape=(jax.ShapeDtypeStruct((3, NODE_DEV // TI...  33.2 us

profile of v6, /device:TPU:1, one launch (start us, length us, event | category | flops | bytes accessed | tf_op | source)
XLA Modules:
  0.0 34.4 jit_solution(8839483027652313647)
XLA Ops:
  0.6 33.2 %segments.1 = (f32[3,4,128]{2,1,0:T(4,128)S(1)}, f32[8,315]{1,0:T(8,128)S(1)}) custom-call(f32[3,32,128]{2,1,0:T(8,128)} %bitcast.17, f32[3,32,128]{2,1,0:T(8,128)} %bitcast.18, f32[3,32,128]{2,1,0:T(8,128)} %bitcast.19, s32[32,128]{1,0:T(8,128)} %bitcast.21, s32[32,2,128]{2,1,0:T(2,128)} %bitcast.20, s32[2,8]{1,0:T(2,128)} %bitcast.23, ...), custom_call_target="tpu_custom_call" | custom-call | tf_op jit(solution)/shard_map/segments/pallas_call | solution.py:475
  33.8 0.6 %outputs.1 = (f32[3,4,128]{2,1,0:T(4,128)}, f32[8,315]{1,0:T(8,128)}) custom-call(f32[3,4,128]{2,1,0:T(4,128)S(1)} %get-tuple-element.6.node_in, f32[8,315]{1,0:T(8,128)S(1)} %get-tuple-element.7.moments_in), custom_call_target="tpu_custom_call" | custom-call | tf_op jit(solution)/shard_map/outputs/pallas_call | solution.py:525
